TPU v7x, 128 devices: a whole 4x4x4 slice. The times are simulated.
128 devices in a mesh: graph: 1, col: 16 (over z, y), row: 8 (over x, core).
Axes of the slice: x: 4, y: 4, z: 4, core: 2. Of those that a mesh axis runs over, the one named last changes fastest.
Arguments:
- flow_init: float32 [8192, 8192], P(('graph', 'row'), 'col')
- flow_graph: float32 [8192, 8192], P(('graph', 'row'), 'col')
Outputs:
- output: float32 [8192, 8192], P(('graph', 'row'), 'col')
All inputs are finite; a program needn't handle non-finite values.
Results may differ from a plain program's by a relative error of at most 0.001.
Values are sent between devices in bfloat16 or wider.
A program may use at most 1 GiB of HBM per device.

v0:
```python
import jax
import jax.numpy as jnp
from jax import lax
from jax.sharding import PartitionSpec as P

ITERATIONS = 3


def solution(mesh):
    num_cols = mesh.shape["col"]
    block_spec = P(("graph", "row"), "col")

    def device_step(init_blk, graph_blk):
        mat_order = init_blk.shape[1] * num_cols
        graph_panel = lax.all_gather(graph_blk.astype(jnp.bfloat16), "row", axis=0, tiled=True)
        flow_blk = init_blk
        for _ in range(ITERATIONS):
            row_panel = lax.all_gather(flow_blk.astype(jnp.bfloat16), "col", axis=1, tiled=True)
            expanded = jnp.dot(row_panel, graph_panel, preferred_element_type=jnp.float32)
            inflated = expanded * expanded
            col_sum = lax.psum(jnp.sum(inflated, axis=0), "row")
            flow_blk = inflated * (mat_order / col_sum)
        return flow_blk

    return jax.shard_map(device_step, mesh=mesh, in_specs=(block_spec, block_spec), out_specs=block_spec, check_vma=False)
```

profile of v0, /device:TPU:1, one launch (start us, length us, event | category | flops | bytes accessed | tf_op | source)
XLA Modules:
  0.0 507.7 jit_solution(11122862538012793862)
XLA Ops:
  6.5 0.0 all-gather.7.cloned.1.call-start
  6.5 2.9 convert_element_type.13
  9.5 0.0 all-gather.7.cloned.1.call-update
  9.5 0.0 all-gather.5.cloned.1.call-start
  9.6 0.0 copy-done
  9.6 1.1 convert_element_type.12
  10.7 0.0 all-gather.5.cloned.1.call-update
  10.7 0.0 all-gather.9.cloned.1.call-start
  10.7 52.0 %all-gather.7.cloned.1.call-done = bf16[8192,512]{1,0:T(8,128)(2,1)} async-done(((bf16[1024,512]{1,0:T(8,128)(2,1)}), bf16[8192,512]{1,0:T(8,128)(2,1)}) %all-gather.7.cloned.1.call-update) | async-done | bytes 8388624 | tf_op jit(solution)/shard_map/all_gather | solution.py:15
  62.7 119.4 %all-gather.5.cloned.1.call-done = bf16[1024,8192]{1,0:T(8,128)(2,1)} async-done(((bf16[1024,512]{1,0:T(8,128)(2,1)}), bf16[1024,8192]{1,0:T(8,128)(2,1)}) %all-gather.5.cloned.1.call-update) | async-done | bytes 16777232 | tf_op jit(solution)/shard_map/all_gather | solution.py:18
  182.2 14.4 %multiply_reduce_fusion.2 = (f32[512]{0:T(512)S(1)}, f32[1024,512]{1,0:T(8,128)S(1)}) fusion(bf16[1024,8192]{1,0:T(8,128)(2,1)} %all-gather.5.cloned.1.call-done, bf16[8192,512]{1,0:T(8,128)(2,1)} %all-gather.7.cloned.1.call-done), kind=kOutput, calls=%fused_computation.5 | convolution fusion | flops 8590983168 | bytes 27265024 | tf_op jit(solution)/shard_map/dot_general | solution.py:19
  196.5 13.9 %psum.21 = f32[512]{0:T(512)S(1)} all-reduce(f32[512]{0:T(512)S(1)} %get-tuple-element.5), channel_id=1, replica_groups=mesh['graph'=1,'col'=16,'row'=8] {'row'}, use_global_device_ids=true, to_apply=%region_1.0 | all-reduce | flops 512 | bytes 4096 | tf_op jit(solution)/shard_map/psum | solution.py:21
  210.4 1.3 multiply_convert_fusion.1
  211.7 0.0 all-gather.9.cloned.1.call-update
  211.7 0.0 all-gather.11.cloned.1.call-start
  211.7 115.0 %all-gather.9.cloned.1.call-done = bf16[1024,8192]{1,0:T(8,128)(2,1)} async-done(((bf16[1024,512]{1,0:T(8,128)(2,1)}), bf16[1024,8192]{1,0:T(8,128)(2,1)}) %all-gather.9.cloned.1.call-update) | async-done | bytes 16777232 | tf_op jit(solution)/shard_map/all_gather | solution.py:18
  326.8 14.4 %multiply_reduce_fusion.1 = (f32[512]{0:T(512)S(1)}, f32[1024,512]{1,0:T(8,128)S(1)}) fusion(bf16[1024,8192]{1,0:T(8,128)(2,1)} %all-gather.9.cloned.1.call-done, bf16[8192,512]{1,0:T(8,128)(2,1)} %all-gather.7.cloned.1.call-done), kind=kOutput, calls=%fused_computation.4 | convolution fusion | flops 8590983168 | bytes 27265024 | tf_op jit(solution)/shard_map/dot_general | solution.py:19
  341.1 13.8 %psum.22 = f32[512]{0:T(512)S(1)} all-reduce(f32[512]{0:T(512)S(1)} %get-tuple-element.7), channel_id=1, replica_groups=mesh['graph'=1,'col'=16,'row'=8] {'row'}, use_global_device_ids=true, to_apply=%region_3.0 | all-reduce | flops 512 | bytes 4096 | tf_op jit(solution)/shard_map/psum | solution.py:21
  355.0 1.3 multiply_convert_fusion
  356.3 0.0 all-gather.11.cloned.1.call-update
  356.3 115.1 %all-gather.11.cloned.1.call-done = bf16[1024,8192]{1,0:T(8,128)(2,1)} async-done(((bf16[1024,512]{1,0:T(8,128)(2,1)}), bf16[1024,8192]{1,0:T(8,128)(2,1)}) %all-gather.11.cloned.1.call-update) | async-done | bytes 16777232 | tf_op jit(solution)/shard_map/all_gather | solution.py:18
  471.4 14.4 %multiply_reduce_fusion = (f32[512]{0:T(512)S(1)}, f32[1024,512]{1,0:T(8,128)S(1)}) fusion(bf16[1024,8192]{1,0:T(8,128)(2,1)} %all-gather.11.cloned.1.call-done, bf16[8192,512]{1,0:T(8,128)(2,1)} %all-gather.7.cloned.1.call-done), kind=kOutput, calls=%fused_computation.3 | convolution fusion | flops 8590983168 | bytes 27265024 | tf_op jit(solution)/shard_map/dot_general | solution.py:19
  485.7 13.8 %psum.23 = f32[512]{0:T(512)S(1)} all-reduce(f32[512]{0:T(512)S(1)} %get-tuple-element.9), channel_id=1, replica_groups=mesh['graph'=1,'col'=16,'row'=8] {'row'}, use_global_device_ids=true, to_apply=%region_5.0 | all-reduce | flops 512 | bytes 4096 | tf_op jit(solution)/shard_map/psum | solution.py:21
  499.6 1.6 multiply_multiply_fusion
  (4 shorter events, 0.0 us)
Async XLA Ops:
  6.5 3.0 copy-start
  6.5 56.2 %all-gather.7.cloned.1.call-start = ((), (), s32[]{:S(2)}) async-start(), calls=%async_computation.1 | async-start | bytes 9437184 | tf_op jit(solution)/shard_map/all_gather | solution.py:15
  9.5 172.7 %all-gather.5.cloned.1.call-start = ((), (), s32[]{:S(2)}) async-start(), calls=%async_computation | async-start | bytes 17825792 | tf_op jit(solution)/shard_map/all_gather | solution.py:18
  10.7 316.1 %all-gather.9.cloned.1.call-start = ((), (), s32[]{:S(2)}) async-start(), calls=%async_computation.2 | async-start | bytes 17825792 | tf_op jit(solution)/shard_map/all_gather | solution.py:18
  211.7 259.7 %all-gather.11.cloned.1.call-start = ((), (), s32[]{:S(2)}) async-start(), calls=%async_computation.3 | async-start | bytes 17825792 | tf_op jit(solution)/shard_map/all_gather | solution.py:18
Sparse Core Ops, SparseCore 0:
  9.6 53.0 all-gather.6
  64.8 117.2 all-gather.4
  211.8 114.9 all-gather.8
  356.4 114.9 all-gather.10
where the time goes:
time: 508 us
  waiting for transfers between devices  402 us (79%)
  matrix products  43.1 us (8%)
  blocking collectives  41.5 us (8%)
  between operations  13.2 us (3%)
  other arithmetic  8.18 us (2%)
    all_gather x3, waiting for transfers between devices, device_step(): lax.all_gather(flow_blk.astype(jnp.bfloat16), 'col', axis=1, tiled=True)  350 us
    all_gather x1, waiting for transfers between devices, device_step(): lax.all_gather(graph_blk.astype(jnp.bfloat16), 'row', axis=0, tiled=True)  52 us
    dot_general x3, matrix products, device_step(): jnp.dot(row_panel, graph_panel, preferred_element_type=jnp.float32)  43.1 us
    psum x3, blocking collectives, device_step(): col_sum = lax.psum(jnp.sum(inflated, axis=0), 'row')  41.5 us
  transfers between devices with their start and end apart: 4, of which 4 were waited for; matrix products, arithmetic and copies ran while one was open for 0% of the time, Pallas kernels for 0%

commit v1 on v0

v1 whole, which is shorter than its diff:
```python
import functools

import jax
import jax.numpy as jnp
from jax import lax
from jax.experimental import pallas as pl
from jax.experimental.pallas import tpu as pltpu
from jax.sharding import PartitionSpec as P

MESH = pl.DeviceIdType.MESH
BF = jnp.bfloat16
F32 = jnp.float32
N = 8192
PLANE, PIECE, BLK, ROWS, LANE = 2048, 1024, 512, 256, 128
XM, XP, YP = 224, 448, 736
ROWS3 = ((0, 64), (64, 64), (128, 64), (192, 64))


def mcl_kernel(
    init_ref, graph_ref, out_ref,
    g, a, stage, acc1, acc2, moved, got, s1a, s2a, s1b, s2b,
    g_send, g_recv, d_recv, t_send, t_recv, az_send, az_recv, az2_recv,
    a1_send, a1_recv, a1_recv2, a2_send, a2_recv, a2_recv2,
    r_send, r_recv1, r_recv2, o_send, o_recv,
):
    col, row = lax.axis_index("col"), lax.axis_index("row")
    z, y = lax.div(col, 4), lax.rem(col, 4)
    x, c = lax.div(row, 2), lax.rem(row, 2)

    def plus(v, d):
        return lax.rem(v + d, 4)

    def dev(dx=0, dy=0, dz=0, dc=0):
        return {"col": plus(z, dz) * 4 + plus(y, dy), "row": plus(x, dx) * 2 + lax.rem(c + dc, 2)}

    XPOS, XNEG, YPOS, YNEG = dev(dx=1), dev(dx=3), dev(dy=1), dev(dy=3)
    ZPOS, ZNEG, MATE = dev(dz=1), dev(dz=3), dev(dc=1)

    def send(src, dst, ssem, rsem, device):
        pltpu.make_async_remote_copy(
            src_ref=src, dst_ref=dst, send_sem=ssem, recv_sem=rsem, device_id=device, device_id_type=MESH
        ).start()

    def await_recv(ref, sem):
        pltpu.make_async_remote_copy(
            src_ref=ref, dst_ref=ref, send_sem=sem, recv_sem=sem, device_id=MATE, device_id_type=MESH
        ).wait_recv()

    def await_send(ref, sem):
        pltpu.make_async_remote_copy(
            src_ref=ref, dst_ref=ref, send_sem=sem, recv_sem=sem, device_id=MATE, device_id_type=MESH
        ).wait_send()

    barrier = pltpu.get_barrier_semaphore()
    peers = [dev(dx=dx, dc=dc) for dx in range(4) for dc in range(2) if (dx, dc) != (0, 0)]
    peers += [dev(dy=dy) for dy in (1, 2, 3)] + [ZPOS, ZNEG]
    for peer in peers:
        pl.semaphore_signal(barrier, inc=1, device_id=peer, device_id_type=MESH)

    def cast_graph(q):
        base = pl.multiple_of((x * 2 + c) * PIECE, PIECE)
        for qr in range(4):
            for yy in range(2):
                g[q, y, pl.ds(base + qr * ROWS + yy * LANE, LANE), :] = graph_ref[
                    pl.ds(yy * BLK + qr * LANE, LANE), pl.ds(q * LANE, LANE)
                ].astype(BF)

    own_rows = pl.ds(pl.multiple_of(y * ROWS, ROWS), ROWS)
    for q in range(4):
        a[0, z, lax.div(y, 2), q, lax.rem(y, 2)] = init_ref[own_rows, pl.ds(q * LANE, LANE)].astype(BF)
    for t in range(4):
        for q in range(4):
            stage[t, q] = init_ref[pl.ds(t * ROWS, ROWS), pl.ds(q * LANE, LANE)].astype(BF)
    cast_graph(0)
    pl.semaphore_wait(barrier, len(peers))

    def a0_block(dz, dy, lo=0, n=4):
        yy = plus(y, dy)
        return a.at[0, plus(z, dz), lax.div(yy, 2), pl.ds(lo, n), lax.rem(yy, 2)]

    def a0_spread(group, dys):
        for dy in dys:
            for where in (ZPOS, ZNEG):
                send(a0_block(0, dy), a0_block(0, dy), az_send, az_recv.at[group], where)

    def a0_relay(group, dys):
        await_recv(a.at[0, 0, pl.ds(0, len(dys))], az_recv.at[group])
        for dy in dys:
            send(a0_block(3, dy, 0, 2), a0_block(3, dy, 0, 2), az_send, az2_recv, ZPOS)
            send(a0_block(1, dy, 2, 2), a0_block(1, dy, 2, 2), az_send, az2_recv, ZNEG)

    def a0_exchange():
        for dy in (1, 3, 2):
            send(stage.at[plus(y, dy)], a0_block(0, 0), t_send, t_recv.at[dy - 1], dev(dy=dy))

    def piece(q, dx, dy, lo=0, hi=PIECE):
        base = (plus(x, dx) * 2 + c) * PIECE
        return g.at[q, plus(y, dy), pl.ds(pl.multiple_of(base + lo, 32), hi - lo), :]

    def hop(q, depth, where, dx, dy, lo=0, hi=PIECE):
        ref = piece(q, dx, dy, lo, hi)
        send(ref, ref, g_send.at[q], g_recv.at[q, depth], where)

    def mate(q, *offsets):
        for dx, dy in offsets:
            ref = piece(q, dx, dy)
            send(ref, ref, g_send.at[q], d_recv.at[q], MATE)

    def arrived(q, depth):
        rows = (4096, 2 * (BLK + 2 * (PIECE - XP)) + 2 * (BLK + 2 * XP), 4096, PIECE)[depth]
        await_recv(g.at[q, 0, pl.ds(0, rows), :], g_recv.at[q, depth])

    def g1(q):
        for where in (XPOS, XNEG, YPOS, YNEG):
            hop(q, 0, where, 0, 0)
        mate(q, (0, 0))

    def g2(q):
        arrived(q, 0)
        hop(q, 1, XPOS, 3, 0, XM, YP)
        hop(q, 1, YPOS, 0, 3, XM, YP)
        for lo, hi in ((0, XM), (YP, PIECE)):
            hop(q, 1, XNEG, 1, 0, lo, hi)
            hop(q, 1, YNEG, 0, 1, lo, hi)
        for d in (1, 3):
            for where in (XPOS, XNEG):
                hop(q, 1, where, 0, d, XP, PIECE)
            for where in (YPOS, YNEG):
                hop(q, 1, where, d, 0, 0, XP)
        mate(q, (1, 0), (3, 0), (0, 1), (0, 3))

    def g3(q):
        arrived(q, 1)
        for where in (XPOS, XNEG):
            hop(q, 2, where, 0, 2, XP, PIECE)
        for where in (YPOS, YNEG):
            hop(q, 2, where, 2, 0, 0, XP)
        for d in (1, 3):
            hop(q, 2, XPOS, 3, d, XP, YP)
            hop(q, 2, XNEG, 1, d, YP, PIECE)
            hop(q, 2, YPOS, d, 3, XM, XP)
            hop(q, 2, YNEG, d, 1, 0, XM)
        mate(q, (2, 0), (0, 2), (1, 1), (1, 3), (3, 1), (3, 3))

    def g4(q):
        arrived(q, 2)
        hop(q, 3, XPOS, 3, 2, XP, YP)
        hop(q, 3, XNEG, 1, 2, YP, PIECE)
        hop(q, 3, YPOS, 2, 3, XM, XP)
        hop(q, 3, YNEG, 2, 1, 0, XM)
        mate(q, (1, 2), (3, 2), (2, 1), (2, 3))

    def g5(q):
        arrived(q, 3)
        mate(q, (2, 2))

    def g_whole(q):
        await_recv(g.at[q, pl.ds(0, 2)], d_recv.at[q])

    def g_rows(nq, start, n):
        return jnp.concatenate([g[nq, t, pl.ds(start, n), :] for t in range(4)], axis=1)

    def c1(q):
        def step(zz, carry):
            lhs = jnp.concatenate(
                [a[0, zz, cc, qr, yy] for cc in range(2) for qr in range(4) for yy in range(2)], axis=1
            )
            prod = jnp.dot(lhs, g_rows(q, pl.multiple_of(zz * PLANE, PLANE), PLANE), preferred_element_type=F32)
            acc1[q] = jnp.where(zz == 0, prod, acc1[q] + prod)
            return carry

        acc1[q] = jnp.zeros((ROWS, BLK), F32)
        lax.fori_loop(0, 4, step, 0)

    def square_sum(ref, q):
        v = ref[q]
        return jnp.sum(v * v, axis=0, keepdims=True)

    def sum_first(s1, i, k):
        me = x * 2 + c
        for dx in range(4):
            for dc in range(2):
                if (dx, dc) != (0, 0):
                    send(s1.at[i, me], s1.at[i, me], r_send.at[0, k], r_recv1.at[k], dev(dx=dx, dc=dc))

    def sum_second(s1, s2, i, k):
        await_recv(s1.at[i, pl.ds(0, 7)], r_recv1.at[k])
        s2[i, y] = jnp.sum(s1[i], axis=0)
        for dy in (1, 2, 3):
            send(s2.at[i, y], s2.at[i, y], r_send.at[1, k], r_recv2.at[k], dev(dy=dy))

    def sum_last(s2, i, k):
        await_recv(s2.at[i, pl.ds(0, 3)], r_recv2.at[k])

    def c1_sums(q):
        s1a[q, x * 2 + c] = square_sum(acc1, q)
        sum_first(s1a, q, q)

    def c1_second(q):
        sum_second(s1a, s2a, q, q)

    def a1_chunk(dz, q, lo=0, n=2):
        return a.at[1, plus(z, dz), pl.ds(lo, n), q]

    def a1_spread(q):
        sum_last(s2a, q, q)
        scale = N / jnp.sum(s2a[q], axis=0)
        for t in range(4):
            v = acc1[q, :, pl.ds(t * LANE, LANE)]
            a[1, z, t // 2, q, t % 2] = (v * v * scale[:, t * LANE : t * LANE + LANE]).astype(BF)
        for where in (ZPOS, ZNEG):
            send(a1_chunk(0, q), a1_chunk(0, q), a1_send, a1_recv.at[q], where)

    def a1_relay(q):
        await_recv(a.at[1, 0, :, pl.ds(0, 2)], a1_recv.at[q])
        send(a1_chunk(3, q, 0, 1), a1_chunk(3, q, 0, 1), a1_send, a1_recv2.at[q], ZPOS)
        send(a1_chunk(1, q, 1, 1), a1_chunk(1, q, 1, 1), a1_send, a1_recv2.at[q], ZNEG)

    def c2(q, dz, first=False):
        zz = plus(z, dz)
        lhs = jnp.concatenate([a[1, zz, cc, q, yy] for cc in range(2) for yy in range(2)], axis=1)
        base = pl.multiple_of(zz * PLANE, PLANE)
        for nq in range(4):
            rhs = jnp.concatenate([g_rows(nq, base + cc * PIECE + q * ROWS, ROWS) for cc in range(2)], axis=0)
            prod = jnp.dot(lhs, rhs, preferred_element_type=F32)
            acc2[nq] = prod if first else acc2[nq] + prod

    def c2_near(q):
        for dz in (1, 3):
            c2(q, dz)

    def c2_far(q):
        await_recv(a.at[1, 0, :, 0], a1_recv2.at[q])
        c2(q, 2)

    def c2_sums():
        for q in range(4):
            s1b[0, x * 2 + c, :, pl.ds(q * BLK, BLK)] = square_sum(acc2, q)
        sum_first(s1b, 0, 4)

    def c2_second():
        sum_second(s1b, s2b, 0, 4)

    def a2_rows(dz, p, lo=0, n=2):
        start, rows = ROWS3[p]
        return a.at[2, plus(z, dz), pl.ds(lo, n), :, :, pl.ds(start, rows), :]

    def a2_spread(p):
        start, rows = ROWS3[p]
        scale = N / jnp.sum(s2b[0], axis=0)
        for q in range(4):
            for t in range(4):
                v = acc2[q, pl.ds(start, rows), pl.ds(t * LANE, LANE)]
                s = scale[:, q * BLK + t * LANE : q * BLK + t * LANE + LANE]
                a[2, z, t // 2, q, t % 2, pl.ds(start, rows), :] = (v * v * s).astype(BF)
        for where in (ZPOS, ZNEG):
            send(a2_rows(0, p), a2_rows(0, p), a2_send.at[p], a2_recv.at[p], where)

    def a2_relay(p):
        start, rows = ROWS3[p]
        await_recv(a.at[2, pl.ds(0, 2), :, :, :, pl.ds(start, rows), :], a2_recv.at[p])
        send(a2_rows(3, p, 0, 1), a2_rows(3, p, 0, 1), a2_send.at[p], a2_recv2.at[p], ZPOS)
        send(a2_rows(1, p, 1, 1), a2_rows(1, p, 1, 1), a2_send.at[p], a2_recv2.at[p], ZNEG)

    def c3_part(zz, start, rows, nq):
        lhs = jnp.concatenate(
            [a[2, zz, cc, qr, yy, pl.ds(start, rows), :] for cc in range(2) for qr in range(4) for yy in range(2)],
            axis=1,
        )
        return jnp.dot(lhs, g_rows(nq, pl.multiple_of(zz * PLANE, PLANE), PLANE), preferred_element_type=F32)

    def c3_own():
        def step(nq, carry):
            acc1[nq] = c3_part(z, 0, ROWS, nq)
            return carry

        lax.fori_loop(0, 4, step, 0)

    def c3_near(p):
        start, rows = ROWS3[p]

        def step(nq, carry):
            acc1[nq, pl.ds(start, rows), :] += c3_part(plus(z, 1), start, rows, nq)
            acc1[nq, pl.ds(start, rows), :] += c3_part(plus(z, 3), start, rows, nq)
            return carry

        lax.fori_loop(0, 4, step, 0)

    def c3_far(p):
        start, rows = ROWS3[p]
        await_recv(a.at[2, 0, :, :, :, pl.ds(start, rows), :], a2_recv2.at[p])
        for nq in range(4):
            v = acc1[nq, pl.ds(start, rows), :] + c3_part(plus(z, 2), start, rows, nq)
            v = v * v
            part = jnp.sum(v, axis=0, keepdims=True)
            lanes = pl.ds(nq * BLK, BLK)
            if p == 0:
                s1b[1, x * 2 + c, :, lanes] = part
            else:
                s1b[1, x * 2 + c, :, lanes] += part
            for t in range(4):
                moved[t, pl.ds(start, rows), pl.ds(nq * LANE, LANE)] = v[:, t * LANE : t * LANE + LANE]
        for dy in (2, 1, 3):
            send(
                moved.at[plus(y, dy), pl.ds(start, rows), :],
                got.at[y, pl.ds(start, rows), :],
                o_send, o_recv, dev(dy=dy),
            )

    def finish():
        await_recv(got.at[pl.ds(0, 3)], o_recv)
        for nq in range(4):
            lanes = pl.ds(pl.multiple_of(nq * BLK + y * LANE, LANE), LANE)
            scale = N / jnp.sum(s2b[1, :, :, lanes], axis=0)
            here = pl.ds(nq * LANE, LANE)
            for dy in range(4):
                t = plus(y, dy)
                v = got[t, :, here] if dy else moved[t, :, here]
                out_ref[pl.ds(pl.multiple_of(t * ROWS, ROWS), ROWS), here] = v * scale

    a0_spread(0, (0,))
    a0_exchange()
    g1(0)
    cast_graph(1)
    g1(1)
    await_recv(stage.at[0], t_recv.at[0])
    await_recv(stage.at[0], t_recv.at[2])
    a0_spread(1, (1, 3))
    await_recv(stage.at[0], t_recv.at[1])
    a0_spread(2, (2,))
    a0_relay(0, (0,))
    cast_graph(2)
    cast_graph(3)
    g2(0)
    g1(2)
    a0_relay(1, (1, 3))
    g2(1)
    g3(0)
    g1(3)
    a0_relay(2, (2,))
    g2(2)
    g3(1)
    g4(0)
    await_recv(a.at[0, 0], az2_recv)
    g5(0)
    g_whole(0)
    c1(0)
    c1_sums(0)
    g2(3)
    g3(2)
    g4(1)
    c1_second(0)
    g5(1)
    g_whole(1)
    c1(1)
    c1_sums(1)
    a1_spread(0)
    g3(3)
    g4(2)
    a1_relay(0)
    c1_second(1)
    g5(2)
    g_whole(2)
    g4(3)
    a1_spread(1)
    c1(2)
    c1_sums(2)
    a1_relay(1)
    c1_second(2)
    g5(3)
    a1_spread(2)
    g_whole(3)
    c1(3)
    c1_sums(3)
    a1_relay(2)
    c2(0, 0, first=True)
    c2(1, 0)
    c1_second(3)
    c2(2, 0)
    a1_spread(3)
    c2(3, 0)
    for q in (0, 1, 2):
        c2_near(q)
        c2_far(q)
    a1_relay(3)
    c2_near(3)
    c2_far(3)
    c2_sums()
    c2_second()
    sum_last(s2b, 0, 4)
    for p in range(4):
        a2_spread(p)
    c3_own()
    for p in range(4):
        a2_relay(p)
        c3_near(p)
        c3_far(p)
    sum_first(s1b, 1, 5)
    sum_second(s1b, s2b, 1, 5)
    sum_last(s2b, 1, 5)
    finish()

    for q in range(4):
        await_send(g.at[q, :, pl.ds(0, 7936), :], g_send.at[q])
    await_send(stage.at[pl.ds(0, 3)], t_send)
    await_send(a.at[0, pl.ds(0, 3)], az_send)
    await_send(a.at[1, pl.ds(0, 3)], a1_send)
    for p, (start, rows) in enumerate(ROWS3):
        await_send(a.at[2, pl.ds(0, 3), :, :, :, pl.ds(start, rows), :], a2_send.at[p])
    for s1, s2, base in ((s1a, s2a, 0), (s1b, s2b, 4)):
        for i in range(s1.shape[0]):
            await_send(s1.at[i, pl.ds(0, 7)], r_send.at[0, base + i])
            await_send(s2.at[i, pl.ds(0, 3)], r_send.at[1, base + i])
    await_send(got.at[pl.ds(0, 3)], o_send)


def solution(mesh):
    block_spec = P(("graph", "row"), "col")
    vmem = pl.BlockSpec(memory_space=pltpu.VMEM)
    dma = pltpu.SemaphoreType.DMA

    def device_step(init_blk, graph_blk):
        return pl.pallas_call(
            mcl_kernel,
            out_shape=jax.ShapeDtypeStruct((PIECE, BLK), F32),
            in_specs=[vmem, vmem],
            out_specs=vmem,
            scratch_shapes=[
                pltpu.VMEM((4, 4, N, LANE), BF),
                pltpu.VMEM((3, 4, 2, 4, 2, ROWS, LANE), BF),
                pltpu.VMEM((4, 4, ROWS, LANE), BF),
                pltpu.VMEM((4, ROWS, BLK), F32),
                pltpu.VMEM((4, ROWS, BLK), F32),
                pltpu.VMEM((4, ROWS, BLK), F32),
                pltpu.VMEM((4, ROWS, BLK), F32),
                pltpu.VMEM((4, 8, 1, BLK), F32),
                pltpu.VMEM((4, 4, 1, BLK), F32),
                pltpu.VMEM((2, 8, 1, PLANE), F32),
                pltpu.VMEM((2, 4, 1, PLANE), F32),
                dma((4,)), dma((4, 4)), dma((4,)),
                dma(()), dma((3,)),
                dma(()), dma((3,)), dma(()),
                dma(()), dma((4,)), dma((4,)),
                dma((4,)), dma((4,)), dma((4,)),
                dma((2, 6)), dma((6,)), dma((6,)),
                dma(()), dma(()),
            ],
            compiler_params=pltpu.CompilerParams(
                collective_id=0, has_side_effects=True, vmem_limit_bytes=67043328
            ),
        )(init_blk, graph_blk)

    return jax.shard_map(device_step, mesh=mesh, in_specs=(block_spec, block_spec), out_specs=block_spec, check_vma=False)
```

time: 508 us -> 224 us (0.44)
  waiting for transfers between devices: 402 us -> 0 us
  Pallas kernels: 0 us -> 221 us
  matrix products: 43.1 us -> 0 us
  blocking collectives: 41.5 us -> 0 us
  between operations: 13.2 us -> 0.01 us
  other arithmetic: 8.18 us -> 0 us
    all_gather x4 -> x0, waiting for transfers between devices: 402 us -> none  [the longest x3 350 us: device_step(): lax.all_gather(flow_blk.astype(jnp.bfloat16), 'col', axis=1, tiled=True)]
    pallas_call x0 -> x1, Pallas kernels: none -> 221 us  [device_step(): pl.pallas_call(mcl_kernel, out_shape=jax.ShapeDtypeStruct((PIECE, BLK), F...]
    dot_general x3 -> x0, matrix products: 43.1 us -> none  [device_step(): jnp.dot(row_panel, graph_panel, preferred_element_type=jnp.float32)]
    psum x3 -> x0, blocking collectives: 41.5 us -> none  [device_step(): col_sum = lax.psum(jnp.sum(inflated, axis=0), 'row')]
    convert_element_type x4 -> x0, other arithmetic: 6.56 us -> none  [the longest x3 3.62 us: device_step(): flow_blk.astype(jnp.bfloat16)]
  transfers between devices with their start and end apart: 4 -> 0, of which waited for: 4 -> 0; matrix products, arithmetic and copies ran while one was open for 0% -> 0% of each run, Pallas kernels for 0% -> 0%
where the time goes in v1:
time: 224 us
  Pallas kernels  221 us (99%)
  local copies, waits for them, and re-layouts  3.08 us (1%)
    pallas_call x1, Pallas kernels, device_step(): pl.pallas_call(mcl_kernel, out_shape=jax.ShapeDtypeStruct((PIECE, BLK), F...  221 us

profile of v1, /device:TPU:1, one launch (start us, length us, event | category | flops | bytes accessed | tf_op | source)
XLA Modules:
  0.0 223.9 jit_solution(7931484170218929530)
XLA Ops:
  0.0 220.8 %shard_map.28 = f32[1024,512]{1,0:T(8,128)} custom-call(f32[1024,512]{1,0:T(8,128)} %init_ref.1, f32[1024,512]{1,0:T(8,128)} %graph_ref.1), custom_call_target="tpu_custom_call" | custom-call | tf_op jit(solution)/shard_map/pallas_call | solution.py:423
  220.8 3.1 %copy.4 = f32[1024,512]{1,0:T(8,128)} copy(f32[1024,512]{1,0:T(8,128)} %shard_map.28) | data formatting | bytes 4194304

commit v2 on v1

--- a/solution.py
+++ b/solution.py
@@ -12,16 +12,20 @@
 F32 = jnp.float32
 N = 8192
 PLANE, PIECE, BLK, ROWS, LANE = 2048, 1024, 512, 256, 128
-XM, XP, YP = 224, 448, 736
-ROWS3 = ((0, 64), (64, 64), (128, 64), (192, 64))
+Q = 4
+Q0, Q1, Q2, Q3 = range(Q)
+NEAR = (1, 3)
+XM, XP, YP = 288, 448, 752
+ROWS3 = ((0, 80), (80, 64), (144, 64), (208, 48))
 
 
 def mcl_kernel(
-    init_ref, graph_ref, out_ref,
+    init_hbm, graph_hbm, out_hbm, scale_ref,
+    init_ref, graph_ref,
     g, a, stage, acc1, acc2, moved, got, s1a, s2a, s1b, s2b,
     g_send, g_recv, d_recv, t_send, t_recv, az_send, az_recv, az2_recv,
     a1_send, a1_recv, a1_recv2, a2_send, a2_recv, a2_recv2,
-    r_send, r_recv1, r_recv2, o_send, o_recv,
+    r_send, r_recv1, r_recv2, o_send, o_recv, i_sem, w_sem,
 ):
     col, row = lax.axis_index("col"), lax.axis_index("row")
     z, y = lax.div(col, 4), lax.rem(col, 4)
@@ -52,24 +56,33 @@
         ).wait_send()
 
     barrier = pltpu.get_barrier_semaphore()
-    peers = [dev(dx=dx, dc=dc) for dx in range(4) for dc in range(2) if (dx, dc) != (0, 0)]
+    peers = [dev(dx=dx, dc=dc) for dx in range(Q) for dc in range(2) if (dx, dc) != (0, 0)]
     peers += [dev(dy=dy) for dy in (1, 2, 3)] + [ZPOS, ZNEG]
     for peer in peers:
         pl.semaphore_signal(barrier, inc=1, device_id=peer, device_id_type=MESH)
 
+    copies = [pltpu.make_async_copy(init_hbm, init_ref, i_sem.at[Q])]
+    for q in range(Q):
+        lanes = pl.ds(q * LANE, LANE)
+        copies.append(pltpu.make_async_copy(graph_hbm.at[:, lanes], graph_ref.at[:, lanes], i_sem.at[q]))
+    for copy in copies:
+        copy.start()
+
     def cast_graph(q):
+        copies[q + 1].wait()
         base = pl.multiple_of((x * 2 + c) * PIECE, PIECE)
-        for qr in range(4):
+        for qr in range(Q):
             for yy in range(2):
                 g[q, y, pl.ds(base + qr * ROWS + yy * LANE, LANE), :] = graph_ref[
                     pl.ds(yy * BLK + qr * LANE, LANE), pl.ds(q * LANE, LANE)
                 ].astype(BF)
 
+    copies[0].wait()
     own_rows = pl.ds(pl.multiple_of(y * ROWS, ROWS), ROWS)
-    for q in range(4):
+    for q in range(Q):
         a[0, z, lax.div(y, 2), q, lax.rem(y, 2)] = init_ref[own_rows, pl.ds(q * LANE, LANE)].astype(BF)
-    for t in range(4):
-        for q in range(4):
+    for t in range(Q):
+        for q in range(Q):
             stage[t, q] = init_ref[pl.ds(t * ROWS, ROWS), pl.ds(q * LANE, LANE)].astype(BF)
     cast_graph(0)
     pl.semaphore_wait(barrier, len(peers))
@@ -82,6 +95,16 @@
         for dy in dys:
             for where in (ZPOS, ZNEG):
                 send(a0_block(0, dy), a0_block(0, dy), az_send, az_recv.at[group], where)
+
+    def a0_wait_near():
+        for k in (0, 2):
+            await_recv(stage.at[0], t_recv.at[k])
+
+    def a0_wait_far():
+        await_recv(stage.at[0], t_recv.at[1])
+
+    def a0_done():
+        await_recv(a.at[0, 0], az2_recv)
 
     def a0_relay(group, dys):
         await_recv(a.at[0, 0, pl.ds(0, len(dys))], az_recv.at[group])
@@ -95,7 +118,7 @@
 
     def piece(q, dx, dy, lo=0, hi=PIECE):
         base = (plus(x, dx) * 2 + c) * PIECE
-        return g.at[q, plus(y, dy), pl.ds(pl.multiple_of(base + lo, 32), hi - lo), :]
+        return g.at[q, plus(y, dy), pl.ds(pl.multiple_of(base + lo, 16), hi - lo), :]
 
     def hop(q, depth, where, dx, dy, lo=0, hi=PIECE):
         ref = piece(q, dx, dy, lo, hi)
@@ -158,12 +181,12 @@
         await_recv(g.at[q, pl.ds(0, 2)], d_recv.at[q])
 
     def g_rows(nq, start, n):
-        return jnp.concatenate([g[nq, t, pl.ds(start, n), :] for t in range(4)], axis=1)
+        return jnp.concatenate([g[nq, t, pl.ds(start, n), :] for t in range(Q)], axis=1)
 
     def c1(q):
         def step(zz, carry):
             lhs = jnp.concatenate(
-                [a[0, zz, cc, qr, yy] for cc in range(2) for qr in range(4) for yy in range(2)], axis=1
+                [a[0, zz, cc, qr, yy] for cc in range(2) for qr in range(Q) for yy in range(2)], axis=1
             )
             prod = jnp.dot(lhs, g_rows(q, pl.multiple_of(zz * PLANE, PLANE), PLANE), preferred_element_type=F32)
             acc1[q] = jnp.where(zz == 0, prod, acc1[q] + prod)
@@ -178,7 +201,7 @@
 
     def sum_first(s1, i, k):
         me = x * 2 + c
-        for dx in range(4):
+        for dx in range(Q):
             for dc in range(2):
                 if (dx, dc) != (0, 0):
                     send(s1.at[i, me], s1.at[i, me], r_send.at[0, k], r_recv1.at[k], dev(dx=dx, dc=dc))
@@ -205,14 +228,15 @@
     def a1_spread(q):
         sum_last(s2a, q, q)
         scale = N / jnp.sum(s2a[q], axis=0)
-        for t in range(4):
+        for t in range(Q):
             v = acc1[q, :, pl.ds(t * LANE, LANE)]
             a[1, z, t // 2, q, t % 2] = (v * v * scale[:, t * LANE : t * LANE + LANE]).astype(BF)
-        for where in (ZPOS, ZNEG):
-            send(a1_chunk(0, q), a1_chunk(0, q), a1_send, a1_recv.at[q], where)
+        for half in range(2):
+            for where, n in ((ZPOS, half), (ZNEG, 1 - half)):
+                send(a1_chunk(0, q, n, 1), a1_chunk(0, q, n, 1), a1_send, a1_recv.at[half, q], where)
 
     def a1_relay(q):
-        await_recv(a.at[1, 0, :, pl.ds(0, 2)], a1_recv.at[q])
+        await_recv(a.at[1, 0, :, 0], a1_recv.at[0, q])
         send(a1_chunk(3, q, 0, 1), a1_chunk(3, q, 0, 1), a1_send, a1_recv2.at[q], ZPOS)
         send(a1_chunk(1, q, 1, 1), a1_chunk(1, q, 1, 1), a1_send, a1_recv2.at[q], ZNEG)
 
@@ -220,13 +244,14 @@
         zz = plus(z, dz)
         lhs = jnp.concatenate([a[1, zz, cc, q, yy] for cc in range(2) for yy in range(2)], axis=1)
         base = pl.multiple_of(zz * PLANE, PLANE)
-        for nq in range(4):
+        for nq in range(Q):
             rhs = jnp.concatenate([g_rows(nq, base + cc * PIECE + q * ROWS, ROWS) for cc in range(2)], axis=0)
             prod = jnp.dot(lhs, rhs, preferred_element_type=F32)
             acc2[nq] = prod if first else acc2[nq] + prod
 
     def c2_near(q):
-        for dz in (1, 3):
+        await_recv(a.at[1, 0, :, 0], a1_recv.at[1, q])
+        for dz in NEAR:
             c2(q, dz)
 
     def c2_far(q):
@@ -234,7 +259,7 @@
         c2(q, 2)
 
     def c2_sums():
-        for q in range(4):
+        for q in range(Q):
             s1b[0, x * 2 + c, :, pl.ds(q * BLK, BLK)] = square_sum(acc2, q)
         sum_first(s1b, 0, 4)
 
@@ -245,26 +270,29 @@
         start, rows = ROWS3[p]
         return a.at[2, plus(z, dz), pl.ds(lo, n), :, :, pl.ds(start, rows), :]
 
-    def a2_spread(p):
+    def a2_scale(p):
         start, rows = ROWS3[p]
         scale = N / jnp.sum(s2b[0], axis=0)
-        for q in range(4):
-            for t in range(4):
+        for q in range(Q):
+            for t in range(Q):
                 v = acc2[q, pl.ds(start, rows), pl.ds(t * LANE, LANE)]
                 s = scale[:, q * BLK + t * LANE : q * BLK + t * LANE + LANE]
                 a[2, z, t // 2, q, t % 2, pl.ds(start, rows), :] = (v * v * s).astype(BF)
-        for where in (ZPOS, ZNEG):
-            send(a2_rows(0, p), a2_rows(0, p), a2_send.at[p], a2_recv.at[p], where)
+
+    def a2_spread(p):
+        for half in range(2):
+            for where, n in ((ZPOS, half), (ZNEG, 1 - half)):
+                send(a2_rows(0, p, n, 1), a2_rows(0, p, n, 1), a2_send.at[p], a2_recv.at[half, p], where)
 
     def a2_relay(p):
         start, rows = ROWS3[p]
-        await_recv(a.at[2, pl.ds(0, 2), :, :, :, pl.ds(start, rows), :], a2_recv.at[p])
+        await_recv(a.at[2, 0, :, :, :, pl.ds(start, rows), :], a2_recv.at[0, p])
         send(a2_rows(3, p, 0, 1), a2_rows(3, p, 0, 1), a2_send.at[p], a2_recv2.at[p], ZPOS)
         send(a2_rows(1, p, 1, 1), a2_rows(1, p, 1, 1), a2_send.at[p], a2_recv2.at[p], ZNEG)
 
     def c3_part(zz, start, rows, nq):
         lhs = jnp.concatenate(
-            [a[2, zz, cc, qr, yy, pl.ds(start, rows), :] for cc in range(2) for qr in range(4) for yy in range(2)],
+            [a[2, zz, cc, qr, yy, pl.ds(start, rows), :] for cc in range(2) for qr in range(Q) for yy in range(2)],
             axis=1,
         )
         return jnp.dot(lhs, g_rows(nq, pl.multiple_of(zz * PLANE, PLANE), PLANE), preferred_element_type=F32)
@@ -278,6 +306,7 @@
 
     def c3_near(p):
         start, rows = ROWS3[p]
+        await_recv(a.at[2, 0, :, :, :, pl.ds(start, rows), :], a2_recv.at[1, p])
 
         def step(nq, carry):
             acc1[nq, pl.ds(start, rows), :] += c3_part(plus(z, 1), start, rows, nq)
@@ -289,7 +318,7 @@
     def c3_far(p):
         start, rows = ROWS3[p]
         await_recv(a.at[2, 0, :, :, :, pl.ds(start, rows), :], a2_recv2.at[p])
-        for nq in range(4):
+        for nq in range(Q):
             v = acc1[nq, pl.ds(start, rows), :] + c3_part(plus(z, 2), start, rows, nq)
             v = v * v
             part = jnp.sum(v, axis=0, keepdims=True)
@@ -298,7 +327,7 @@
                 s1b[1, x * 2 + c, :, lanes] = part
             else:
                 s1b[1, x * 2 + c, :, lanes] += part
-            for t in range(4):
+            for t in range(Q):
                 moved[t, pl.ds(start, rows), pl.ds(nq * LANE, LANE)] = v[:, t * LANE : t * LANE + LANE]
         for dy in (2, 1, 3):
             send(
@@ -307,100 +336,128 @@
                 o_send, o_recv, dev(dy=dy),
             )
 
+    def c3_sums():
+        sum_first(s1b, 1, Q + 1)
+
+    def c3_second():
+        sum_second(s1b, s2b, 1, Q + 1)
+
+    def result_out():
+        await_recv(got.at[pl.ds(0, 3)], o_recv)
+        for dy in range(Q):
+            t = plus(y, dy)
+            ref = (got if dy else moved).at[t]
+            rows = pl.ds(pl.multiple_of(t * ROWS, ROWS), ROWS)
+            outs.append(pltpu.make_async_copy(ref, out_hbm.at[rows, :], w_sem.at[dy]))
+            outs[-1].start()
+
     def finish():
-        await_recv(got.at[pl.ds(0, 3)], o_recv)
-        for nq in range(4):
+        for nq in range(Q):
             lanes = pl.ds(pl.multiple_of(nq * BLK + y * LANE, LANE), LANE)
-            scale = N / jnp.sum(s2b[1, :, :, lanes], axis=0)
-            here = pl.ds(nq * LANE, LANE)
-            for dy in range(4):
-                t = plus(y, dy)
-                v = got[t, :, here] if dy else moved[t, :, here]
-                out_ref[pl.ds(pl.multiple_of(t * ROWS, ROWS), ROWS), here] = v * scale
-
+            scale_ref[:, pl.ds(nq * LANE, LANE)] = N / jnp.sum(s2b[1, :, :, lanes], axis=0)
+        for copy in outs:
+            copy.wait()
+
+    outs = []
+    g1(Q0)
     a0_spread(0, (0,))
+    cast_graph(Q1)
+    g1(Q1)
+    cast_graph(Q2)
+    cast_graph(Q3)
+    g2(Q0)
+    g1(Q2)
     a0_exchange()
-    g1(0)
-    cast_graph(1)
-    g1(1)
-    await_recv(stage.at[0], t_recv.at[0])
-    await_recv(stage.at[0], t_recv.at[2])
-    a0_spread(1, (1, 3))
-    await_recv(stage.at[0], t_recv.at[1])
+    g2(Q1)
+    a0_relay(0, (0,))
+    g3(Q0)
+    g3(Q1)
+    a0_wait_near()
+    a0_spread(1, NEAR)
+    a0_wait_far()
     a0_spread(2, (2,))
-    a0_relay(0, (0,))
-    cast_graph(2)
-    cast_graph(3)
-    g2(0)
-    g1(2)
-    a0_relay(1, (1, 3))
-    g2(1)
-    g3(0)
-    g1(3)
+    g2(Q2)
+    g4(Q0)
+    a0_relay(1, NEAR)
+    g1(Q3)
     a0_relay(2, (2,))
-    g2(2)
-    g3(1)
-    g4(0)
-    await_recv(a.at[0, 0], az2_recv)
-    g5(0)
-    g_whole(0)
-    c1(0)
-    c1_sums(0)
-    g2(3)
-    g3(2)
-    g4(1)
-    c1_second(0)
-    g5(1)
-    g_whole(1)
-    c1(1)
-    c1_sums(1)
-    a1_spread(0)
-    g3(3)
-    g4(2)
-    a1_relay(0)
-    c1_second(1)
-    g5(2)
-    g_whole(2)
-    g4(3)
-    a1_spread(1)
-    c1(2)
-    c1_sums(2)
-    a1_relay(1)
-    c1_second(2)
-    g5(3)
-    a1_spread(2)
-    g_whole(3)
-    c1(3)
-    c1_sums(3)
-    a1_relay(2)
-    c2(0, 0, first=True)
-    c2(1, 0)
-    c1_second(3)
-    c2(2, 0)
-    a1_spread(3)
-    c2(3, 0)
-    for q in (0, 1, 2):
-        c2_near(q)
-        c2_far(q)
-    a1_relay(3)
-    c2_near(3)
-    c2_far(3)
+    g4(Q1)
+    g3(Q2)
+    g5(Q0)
+    g2(Q3)
+    a0_done()
+    g5(Q1)
+    g_whole(Q0)
+    c1(Q0)
+    c1_sums(Q0)
+    g4(Q2)
+    g_whole(Q1)
+    c1_second(Q0)
+    c1(Q1)
+    c1_sums(Q1)
+    a1_spread(Q0)
+    g3(Q3)
+    g5(Q2)
+    c1_second(Q1)
+    a1_relay(Q0)
+    g_whole(Q2)
+    a1_spread(Q1)
+    c1(Q2)
+    c1_sums(Q2)
+    g4(Q3)
+    c1_second(Q2)
+    g5(Q3)
+    a1_relay(Q1)
+    a1_spread(Q2)
+    g_whole(Q3)
+    c1(Q3)
+    c1_sums(Q3)
+    c2(Q0, 0, True)
+    c2(Q1, 0)
+    a1_relay(Q2)
+    c2(Q2, 0)
+    c1_second(Q3)
+    c2_near(Q0)
+    a1_spread(Q3)
+    c2_far(Q0)
+    c2_near(Q1)
+    c2(Q3, 0)
+    a1_relay(Q3)
+    c2_far(Q1)
+    c2_near(Q2)
+    c2_far(Q2)
+    c2_near(Q3)
+    c2_far(Q3)
     c2_sums()
     c2_second()
-    sum_last(s2b, 0, 4)
-    for p in range(4):
-        a2_spread(p)
+    sum_last(s2b, 0, Q)
+    a2_scale(Q0)
+    a2_spread(Q0)
+    for p in (Q1, Q2, Q3):
+        a2_scale(p)
     c3_own()
-    for p in range(4):
-        a2_relay(p)
-        c3_near(p)
-        c3_far(p)
-    sum_first(s1b, 1, 5)
-    sum_second(s1b, s2b, 1, 5)
-    sum_last(s2b, 1, 5)
+    a2_relay(Q0)
+    a2_spread(Q1)
+    c3_near(Q0)
+    c3_far(Q0)
+    a2_relay(Q1)
+    a2_spread(Q2)
+    c3_near(Q1)
+    c3_far(Q1)
+    a2_relay(Q2)
+    a2_spread(Q3)
+    c3_near(Q2)
+    c3_far(Q2)
+    a2_relay(Q3)
+    c3_near(Q3)
+    c3_far(Q3)
+    c3_sums()
+    c3_second()
+    result_out()
+    sum_last(s2b, 1, Q + 1)
     finish()
 
-    for q in range(4):
+    for q in range(Q):
         await_send(g.at[q, :, pl.ds(0, 7936), :], g_send.at[q])
     await_send(stage.at[pl.ds(0, 3)], t_send)
     await_send(a.at[0, pl.ds(0, 3)], az_send)
@@ -416,16 +473,17 @@
 
 def solution(mesh):
     block_spec = P(("graph", "row"), "col")
-    vmem = pl.BlockSpec(memory_space=pltpu.VMEM)
+    hbm = pl.BlockSpec(memory_space=pl.ANY)
     dma = pltpu.SemaphoreType.DMA
 
     def device_step(init_blk, graph_blk):
-        return pl.pallas_call(
+        moved, scale = pl.pallas_call(
             mcl_kernel,
-            out_shape=jax.ShapeDtypeStruct((PIECE, BLK), F32),
-            in_specs=[vmem, vmem],
-            out_specs=vmem,
+            out_shape=(jax.ShapeDtypeStruct((PIECE, BLK), F32), jax.ShapeDtypeStruct((1, BLK), F32)),
+            in_specs=[hbm, hbm],
+            out_specs=(hbm, pl.BlockSpec(memory_space=pltpu.VMEM)),
             scratch_shapes=[
+                pltpu.VMEM((PIECE, BLK), F32), pltpu.VMEM((PIECE, BLK), F32),
                 pltpu.VMEM((4, 4, N, LANE), BF),
                 pltpu.VMEM((3, 4, 2, 4, 2, ROWS, LANE), BF),
                 pltpu.VMEM((4, 4, ROWS, LANE), BF),
@@ -440,14 +498,16 @@
                 dma((4,)), dma((4, 4)), dma((4,)),
                 dma(()), dma((3,)),
                 dma(()), dma((3,)), dma(()),
-                dma(()), dma((4,)), dma((4,)),
-                dma((4,)), dma((4,)), dma((4,)),
+                dma(()), dma((2, Q)), dma((Q,)),
+                dma((Q,)), dma((2, Q)), dma((Q,)),
                 dma((2, 6)), dma((6,)), dma((6,)),
                 dma(()), dma(()),
+                dma((Q + 1,)), dma((Q,)),
             ],
             compiler_params=pltpu.CompilerParams(
                 collective_id=0, has_side_effects=True, vmem_limit_bytes=67043328
             ),
         )(init_blk, graph_blk)
+        return moved * scale
 
     return jax.shard_map(device_step, mesh=mesh, in_specs=(block_spec, block_spec), out_specs=block_spec, check_vma=False)

time: 224 us -> 196 us (0.88)
  Pallas kernels: 221 us -> 192 us
  other arithmetic: 0 us -> 3.16 us
  local copies, waits for them, and re-layouts: 3.08 us -> 0 us
    pallas_call x1, Pallas kernels: 221 us -> 192 us  [device_step(): pl.pallas_call(mcl_kernel, out_shape=(jax.ShapeDtypeStruct((PIECE, BLK),...]
    mul x0 -> x1, other arithmetic: none -> 3.16 us  [device_step(): return moved * scale]
    unnamed x1 -> x0, local copies, waits for them, and re-layouts: 3.08 us -> none
where the time goes in v2:
time: 196 us
  Pallas kernels  192 us (98%)
  other arithmetic  3.16 us (2%)
    pallas_call x1, Pallas kernels, device_step(): pl.pallas_call(mcl_kernel, out_shape=(jax.ShapeDtypeStruct((PIECE, BLK),...  192 us

profile of v2, /device:TPU:1, one launch (start us, length us, event | category | flops | bytes accessed | tf_op | source)
XLA Modules:
  0.0 195.7 jit_solution(14506352496533232525)
XLA Ops:
  0.0 192.5 %shard_map.28 = (f32[1024,512]{1,0:T(8,128)}, f32[1,512]{1,0:T(1,128)}) custom-call(f32[1024,512]{1,0:T(8,128)} %init_hbm.1, f32[1024,512]{1,0:T(8,128)} %graph_hbm.1), custom_call_target="tpu_custom_call" | custom-call | tf_op jit(solution)/shard_map/pallas_call | solution.py:480
  192.5 3.2 %broadcast_multiply_fusion = f32[1024,512]{1,0:T(8,128)} fusion(f32[1024,512]{1,0:T(8,128)} %get-tuple-element.7, f32[512]{0:T(512)} %bitcast.1), kind=kLoop, calls=%fused_computation | loop fusion | flops 524288 | bytes 4196352 | tf_op jit(solution)/shard_map/mul | solution.py:511

commit v3 on v2

--- a/solution.py
+++ b/solution.py
@@ -15,15 +15,15 @@
 Q = 4
 Q0, Q1, Q2, Q3 = range(Q)
 NEAR = (1, 3)
-XM, XP, YP = 288, 448, 752
+XM, XP, YP = 224, 448, 736
 ROWS3 = ((0, 80), (80, 64), (144, 64), (208, 48))
 
 
 def mcl_kernel(
     init_hbm, graph_hbm, out_hbm, scale_ref,
     init_ref, graph_ref,
-    g, a, stage, acc1, acc2, moved, got, s1a, s2a, s1b, s2b,
-    g_send, g_recv, d_recv, t_send, t_recv, az_send, az_recv, az2_recv,
+    g, a, stage, hold, acc1, acc2, moved, got, s1a, s2a, s1b, s2b,
+    g_send, g_recv, d_recv, t_send, t_recv, h_recv, az_send, az_recv, az2_recv,
     a1_send, a1_recv, a1_recv2, a2_send, a2_recv, a2_recv2,
     r_send, r_recv1, r_recv2, o_send, o_recv, i_sem, w_sem,
 ):
@@ -97,11 +97,11 @@
                 send(a0_block(0, dy), a0_block(0, dy), az_send, az_recv.at[group], where)
 
     def a0_wait_near():
-        for k in (0, 2):
+        for k in range(2):
             await_recv(stage.at[0], t_recv.at[k])
 
     def a0_wait_far():
-        await_recv(stage.at[0], t_recv.at[1])
+        await_recv(stage.at[0], t_recv.at[2])
 
     def a0_done():
         await_recv(a.at[0, 0], az2_recv)
@@ -113,8 +113,16 @@
             send(a0_block(1, dy, 2, 2), a0_block(1, dy, 2, 2), az_send, az2_recv, ZNEG)
 
     def a0_exchange():
-        for dy in (1, 3, 2):
-            send(stage.at[plus(y, dy)], a0_block(0, 0), t_send, t_recv.at[dy - 1], dev(dy=dy))
+        far = plus(y, 2)
+        for side, where in enumerate((YPOS, YNEG)):
+            send(stage.at[far, pl.ds(2 * side, 2)], hold.at[side], t_send, h_recv, where)
+            send(stage.at[plus(y, NEAR[side])], a0_block(0, 0), t_send, t_recv.at[side], where)
+
+    def a0_pass():
+        await_recv(hold, h_recv)
+        for side, where in enumerate((YPOS, YNEG)):
+            ref = a0_block(0, NEAR[1 - side], 2 * side, 2)
+            send(hold.at[side], ref, t_send, t_recv.at[2], where)
 
     def piece(q, dx, dy, lo=0, hi=PIECE):
         base = (plus(x, dx) * 2 + c) * PIECE
@@ -124,10 +132,10 @@
         ref = piece(q, dx, dy, lo, hi)
         send(ref, ref, g_send.at[q], g_recv.at[q, depth], where)
 
-    def mate(q, *offsets):
+    def mate(q, *offsets, last=0):
         for dx, dy in offsets:
             ref = piece(q, dx, dy)
-            send(ref, ref, g_send.at[q], d_recv.at[q], MATE)
+            send(ref, ref, g_send.at[q], d_recv.at[last, q], MATE)
 
     def arrived(q, depth):
         rows = (4096, 2 * (BLK + 2 * (PIECE - XP)) + 2 * (BLK + 2 * XP), 4096, PIECE)[depth]
@@ -175,25 +183,33 @@
 
     def g5(q):
         arrived(q, 3)
-        mate(q, (2, 2))
+        mate(q, (2, 2), last=1)
+
+    def g_most(q):
+        await_recv(g.at[q, pl.ds(0, 3), pl.ds(0, 5 * PIECE)], d_recv.at[0, q])
 
     def g_whole(q):
-        await_recv(g.at[q, pl.ds(0, 2)], d_recv.at[q])
+        await_recv(g.at[q, 0, pl.ds(0, PIECE)], d_recv.at[1, q])
 
     def g_rows(nq, start, n):
         return jnp.concatenate([g[nq, t, pl.ds(start, n), :] for t in range(Q)], axis=1)
 
-    def c1(q):
-        def step(zz, carry):
-            lhs = jnp.concatenate(
-                [a[0, zz, cc, qr, yy] for cc in range(2) for qr in range(Q) for yy in range(2)], axis=1
-            )
-            prod = jnp.dot(lhs, g_rows(q, pl.multiple_of(zz * PLANE, PLANE), PLANE), preferred_element_type=F32)
-            acc1[q] = jnp.where(zz == 0, prod, acc1[q] + prod)
+    def c1_part(q, zz):
+        lhs = jnp.concatenate(
+            [a[0, zz, cc, qr, yy] for cc in range(2) for qr in range(Q) for yy in range(2)], axis=1
+        )
+        acc1[q] += jnp.dot(lhs, g_rows(q, pl.multiple_of(zz * PLANE, PLANE), PLANE), preferred_element_type=F32)
+
+    def c1_most(q):
+        def step(i, carry):
+            c1_part(q, plus(x, i + lax.div(i, 2)))
             return carry
 
         acc1[q] = jnp.zeros((ROWS, BLK), F32)
-        lax.fori_loop(0, 4, step, 0)
+        lax.fori_loop(0, 3, step, 0)
+
+    def c1_rest(q):
+        c1_part(q, plus(x, 2))
 
     def square_sum(ref, q):
         v = ref[q]
@@ -361,72 +377,81 @@
     outs = []
     g1(Q0)
     a0_spread(0, (0,))
+    a0_exchange()
+    cast_graph(Q2)
+    g1(Q2)
+    g2(Q0)
+    a0_wait_near()
+    a0_spread(1, NEAR)
     cast_graph(Q1)
     g1(Q1)
-    cast_graph(Q2)
-    cast_graph(Q3)
-    g2(Q0)
-    g1(Q2)
-    a0_exchange()
-    g2(Q1)
+    a0_pass()
+    g2(Q2)
     a0_relay(0, (0,))
     g3(Q0)
-    g3(Q1)
-    a0_wait_near()
-    a0_spread(1, NEAR)
+    g2(Q1)
     a0_wait_far()
     a0_spread(2, (2,))
-    g2(Q2)
+    a0_relay(1, NEAR)
+    cast_graph(Q3)
+    g1(Q3)
     g4(Q0)
-    a0_relay(1, NEAR)
-    g1(Q3)
-    a0_relay(2, (2,))
-    g4(Q1)
+    g3(Q1)
     g3(Q2)
     g5(Q0)
+    g_most(Q0)
+    a0_relay(2, (2,))
+    a0_done()
+    g4(Q1)
+    c1_most(Q0)
     g2(Q3)
-    a0_done()
-    g5(Q1)
     g_whole(Q0)
-    c1(Q0)
+    c1_rest(Q0)
     c1_sums(Q0)
     g4(Q2)
+    g_most(Q1)
+    c1_most(Q1)
+    c1_second(Q0)
+    g5(Q1)
     g_whole(Q1)
-    c1_second(Q0)
-    c1(Q1)
+    c1_rest(Q1)
     c1_sums(Q1)
+    g_most(Q2)
     a1_spread(Q0)
     g3(Q3)
+    a1_relay(Q0)
+    c1_second(Q1)
     g5(Q2)
-    c1_second(Q1)
-    a1_relay(Q0)
+    c1_most(Q2)
     g_whole(Q2)
+    c1_rest(Q2)
+    c1_sums(Q2)
     a1_spread(Q1)
-    c1(Q2)
-    c1_sums(Q2)
     g4(Q3)
     c1_second(Q2)
-    g5(Q3)
     a1_relay(Q1)
     a1_spread(Q2)
+    g_most(Q3)
+    g5(Q3)
+    c1_most(Q3)
     g_whole(Q3)
-    c1(Q3)
+    c1_rest(Q3)
     c1_sums(Q3)
     c2(Q0, 0, True)
-    c2(Q1, 0)
+    c1_second(Q3)
     a1_relay(Q2)
-    c2(Q2, 0)
-    c1_second(Q3)
     c2_near(Q0)
     a1_spread(Q3)
+    c2(Q1, 0)
+    c2_near(Q2)
+    c2_near(Q1)
+    c2_far(Q1)
+    a1_relay(Q3)
+    c2_far(Q2)
+    c2(Q3, 0)
     c2_far(Q0)
-    c2_near(Q1)
-    c2(Q3, 0)
-    a1_relay(Q3)
-    c2_far(Q1)
-    c2_near(Q2)
-    c2_far(Q2)
     c2_near(Q3)
+    c2(Q2, 0)
     c2_far(Q3)
     c2_sums()
     c2_second()
@@ -459,7 +484,7 @@
 
     for q in range(Q):
         await_send(g.at[q, :, pl.ds(0, 7936), :], g_send.at[q])
-    await_send(stage.at[pl.ds(0, 3)], t_send)
+    await_send(stage, t_send)
     await_send(a.at[0, pl.ds(0, 3)], az_send)
     await_send(a.at[1, pl.ds(0, 3)], a1_send)
     for p, (start, rows) in enumerate(ROWS3):
@@ -487,6 +512,7 @@
                 pltpu.VMEM((4, 4, N, LANE), BF),
                 pltpu.VMEM((3, 4, 2, 4, 2, ROWS, LANE), BF),
                 pltpu.VMEM((4, 4, ROWS, LANE), BF),
+                pltpu.VMEM((2, 2, ROWS, LANE), BF),
                 pltpu.VMEM((4, ROWS, BLK), F32),
                 pltpu.VMEM((4, ROWS, BLK), F32),
                 pltpu.VMEM((4, ROWS, BLK), F32),
@@ -495,8 +521,8 @@
                 pltpu.VMEM((4, 4, 1, BLK), F32),
                 pltpu.VMEM((2, 8, 1, PLANE), F32),
                 pltpu.VMEM((2, 4, 1, PLANE), F32),
-                dma((4,)), dma((4, 4)), dma((4,)),
-                dma(()), dma((3,)),
+                dma((Q,)), dma((Q, Q)), dma((2, Q)),
+                dma(()), dma((3,)), dma(()),
                 dma(()), dma((3,)), dma(()),
                 dma(()), dma((2, Q)), dma((Q,)),
                 dma((Q,)), dma((2, Q)), dma((Q,)),

time: 196 us -> 191 us (0.974)
  Pallas kernels: 192 us -> 188 us
    pallas_call x1, Pallas kernels: 192 us -> 188 us  [device_step(): pl.pallas_call(mcl_kernel, out_shape=(jax.ShapeDtypeStruct((PIECE, BLK),...]
where the time goes in v3:
time: 191 us
  Pallas kernels  188 us (98%)
  other arithmetic  3.16 us (2%)
    pallas_call x1, Pallas kernels, device_step(): pl.pallas_call(mcl_kernel, out_shape=(jax.ShapeDtypeStruct((PIECE, BLK),...  188 us

profile of v3, /device:TPU:1, one launch (start us, length us, event | category | flops | bytes accessed | tf_op | source)
XLA Modules:
  0.0 190.8 jit_solution(12845414549785483322)
XLA Ops:
  0.0 187.7 %shard_map.28 = (f32[1024,512]{1,0:T(8,128)}, f32[1,512]{1,0:T(1,128)}) custom-call(f32[1024,512]{1,0:T(8,128)} %init_hbm.1, f32[1024,512]{1,0:T(8,128)} %graph_hbm.1), custom_call_target="tpu_custom_call" | custom-call | tf_op jit(solution)/shard_map/pallas_call | solution.py:505
  187.7 3.2 %broadcast_multiply_fusion = f32[1024,512]{1,0:T(8,128)} fusion(f32[1024,512]{1,0:T(8,128)} %get-tuple-element.7, f32[512]{0:T(512)} %bitcast.1), kind=kLoop, calls=%fused_computation | loop fusion | flops 524288 | bytes 4196352 | tf_op jit(solution)/shard_map/mul | solution.py:537

commit v4 on v3

--- a/solution.py
+++ b/solution.py
@@ -8,6 +8,7 @@
 from jax.sharding import PartitionSpec as P
 
 MESH = pl.DeviceIdType.MESH
+VMEM_BYTES = 58 << 20
 BF = jnp.bfloat16
 F32 = jnp.float32
 N = 8192
@@ -20,12 +21,12 @@
 
 
 def mcl_kernel(
-    init_hbm, graph_hbm, out_hbm, scale_ref,
-    init_ref, graph_ref,
-    g, a, stage, hold, acc1, acc2, moved, got, s1a, s2a, s1b, s2b,
+    init_hbm, graph_hbm, out_ref,
+    moved, got,
+    g, a, stage, hold, acc1, acc2, s1a, s2a, s1b, s2b, s3, s4,
     g_send, g_recv, d_recv, t_send, t_recv, h_recv, az_send, az_recv, az2_recv,
     a1_send, a1_recv, a1_recv2, a2_send, a2_recv, a2_recv2,
-    r_send, r_recv1, r_recv2, o_send, o_recv, i_sem, w_sem,
+    r_send, r_recv1, r_recv2, o_send, o_recv, f_send, f_recv, i_sem,
 ):
     col, row = lax.axis_index("col"), lax.axis_index("row")
     z, y = lax.div(col, 4), lax.rem(col, 4)
@@ -61,30 +62,42 @@
     for peer in peers:
         pl.semaphore_signal(barrier, inc=1, device_id=peer, device_id_type=MESH)
 
-    copies = [pltpu.make_async_copy(init_hbm, init_ref, i_sem.at[Q])]
-    for q in range(Q):
+    init_ref, graph_ref = moved, got
+    copies = []
+    for q in range(Q + 1):
         lanes = pl.ds(q * LANE, LANE)
-        copies.append(pltpu.make_async_copy(graph_hbm.at[:, lanes], graph_ref.at[:, lanes], i_sem.at[q]))
-    for copy in copies:
-        copy.start()
+        parts = []
+        for t in range(Q):
+            rows = pl.ds(t * ROWS, ROWS)
+            if q == Q:
+                parts.append(pltpu.make_async_copy(init_hbm.at[rows], init_ref.at[t], i_sem.at[q, t]))
+            else:
+                parts.append(
+                    pltpu.make_async_copy(graph_hbm.at[rows, lanes], graph_ref.at[t, :, lanes], i_sem.at[q, t])
+                )
+        copies.append(parts)
+    for q in (Q, Q0, Q1, Q2, Q3):
+        for copy in copies[q]:
+            copy.start()
 
     def cast_graph(q):
-        copies[q + 1].wait()
+        for copy in copies[q]:
+            copy.wait()
         base = pl.multiple_of((x * 2 + c) * PIECE, PIECE)
+        lanes = pl.ds(q * LANE, LANE)
         for qr in range(Q):
             for yy in range(2):
-                g[q, y, pl.ds(base + qr * ROWS + yy * LANE, LANE), :] = graph_ref[
-                    pl.ds(yy * BLK + qr * LANE, LANE), pl.ds(q * LANE, LANE)
-                ].astype(BF)
-
-    copies[0].wait()
-    own_rows = pl.ds(pl.multiple_of(y * ROWS, ROWS), ROWS)
+                block = graph_ref[yy * 2 + qr // 2, pl.ds(qr % 2 * LANE, LANE), lanes]
+                g[q, y, pl.ds(base + qr * ROWS + yy * LANE, LANE), :] = block.astype(BF)
+
+    cast_graph(Q0)
+    for copy in copies[Q]:
+        copy.wait()
     for q in range(Q):
-        a[0, z, lax.div(y, 2), q, lax.rem(y, 2)] = init_ref[own_rows, pl.ds(q * LANE, LANE)].astype(BF)
+        a[0, z, lax.div(y, 2), q, lax.rem(y, 2)] = init_ref[y, :, pl.ds(q * LANE, LANE)].astype(BF)
     for t in range(Q):
         for q in range(Q):
-            stage[t, q] = init_ref[pl.ds(t * ROWS, ROWS), pl.ds(q * LANE, LANE)].astype(BF)
-    cast_graph(0)
+            stage[t, q] = init_ref[t, :, pl.ds(q * LANE, LANE)].astype(BF)
     pl.semaphore_wait(barrier, len(peers))
 
     def a0_block(dz, dy, lo=0, n=4):
@@ -338,13 +351,16 @@
             v = acc1[nq, pl.ds(start, rows), :] + c3_part(plus(z, 2), start, rows, nq)
             v = v * v
             part = jnp.sum(v, axis=0, keepdims=True)
-            lanes = pl.ds(nq * BLK, BLK)
-            if p == 0:
-                s1b[1, x * 2 + c, :, lanes] = part
-            else:
-                s1b[1, x * 2 + c, :, lanes] += part
+            here = pl.ds(nq * LANE, LANE)
             for t in range(Q):
-                moved[t, pl.ds(start, rows), pl.ds(nq * LANE, LANE)] = v[:, t * LANE : t * LANE + LANE]
+                cut = slice(t * LANE, t * LANE + LANE)
+                moved[t, pl.ds(start, rows), here] = v[:, cut]
+                if p == 0:
+                    s3[t, :, here] = part[:, cut]
+                else:
+                    s3[t, :, here] += part[:, cut]
+        if p == Q3:
+            c3_sums()
         for dy in (2, 1, 3):
             send(
                 moved.at[plus(y, dy), pl.ds(start, rows), :],
@@ -353,28 +369,23 @@
             )
 
     def c3_sums():
-        sum_first(s1b, 1, Q + 1)
-
-    def c3_second():
-        sum_second(s1b, s2b, 1, Q + 1)
-
-    def result_out():
+        me = y * 8 + x * 2 + c
+        s4[me] = s3[y]
+        for dy in (2, 1, 3, 0):
+            for dx in (2, 1, 3, 0):
+                for dc in range(2):
+                    if dx + dy + dc:
+                        send(s3.at[plus(y, dy)], s4.at[me], f_send, f_recv, dev(dx=dx, dy=dy, dc=dc))
+
+    def finish():
+        await_recv(s4.at[pl.ds(0, 31)], f_recv)
+        scale = N / jnp.sum(s4[...], axis=0)
+        out_ref[y] = moved[y] * scale
         await_recv(got.at[pl.ds(0, 3)], o_recv)
-        for dy in range(Q):
+        for dy in (1, 2, 3):
             t = plus(y, dy)
-            ref = (got if dy else moved).at[t]
-            rows = pl.ds(pl.multiple_of(t * ROWS, ROWS), ROWS)
-            outs.append(pltpu.make_async_copy(ref, out_hbm.at[rows, :], w_sem.at[dy]))
-            outs[-1].start()
-
-    def finish():
-        for nq in range(Q):
-            lanes = pl.ds(pl.multiple_of(nq * BLK + y * LANE, LANE), LANE)
-            scale_ref[:, pl.ds(nq * LANE, LANE)] = N / jnp.sum(s2b[1, :, :, lanes], axis=0)
-        for copy in outs:
-            copy.wait()
-
-    outs = []
+            out_ref[t] = got[t] * scale
+
     g1(Q0)
     a0_spread(0, (0,))
     a0_exchange()
@@ -476,10 +487,6 @@
     a2_relay(Q3)
     c3_near(Q3)
     c3_far(Q3)
-    c3_sums()
-    c3_second()
-    result_out()
-    sum_last(s2b, 1, Q + 1)
     finish()
 
     for q in range(Q):
@@ -494,6 +501,7 @@
             await_send(s1.at[i, pl.ds(0, 7)], r_send.at[0, base + i])
             await_send(s2.at[i, pl.ds(0, 3)], r_send.at[1, base + i])
     await_send(got.at[pl.ds(0, 3)], o_send)
+    await_send(s4.at[pl.ds(0, 31)], f_send)
 
 
 def solution(mesh):
@@ -502,38 +510,37 @@
     dma = pltpu.SemaphoreType.DMA
 
     def device_step(init_blk, graph_blk):
-        moved, scale = pl.pallas_call(
+        result = pl.pallas_call(
             mcl_kernel,
-            out_shape=(jax.ShapeDtypeStruct((PIECE, BLK), F32), jax.ShapeDtypeStruct((1, BLK), F32)),
+            out_shape=pltpu.VMEM((Q, ROWS, BLK), F32),
             in_specs=[hbm, hbm],
-            out_specs=(hbm, pl.BlockSpec(memory_space=pltpu.VMEM)),
+            out_specs=pl.BlockSpec(memory_space=pltpu.VMEM),
             scratch_shapes=[
-                pltpu.VMEM((PIECE, BLK), F32), pltpu.VMEM((PIECE, BLK), F32),
+                pltpu.VMEM((Q, ROWS, BLK), F32), pltpu.VMEM((Q, ROWS, BLK), F32),
                 pltpu.VMEM((4, 4, N, LANE), BF),
                 pltpu.VMEM((3, 4, 2, 4, 2, ROWS, LANE), BF),
                 pltpu.VMEM((4, 4, ROWS, LANE), BF),
                 pltpu.VMEM((2, 2, ROWS, LANE), BF),
                 pltpu.VMEM((4, ROWS, BLK), F32),
                 pltpu.VMEM((4, ROWS, BLK), F32),
-                pltpu.VMEM((4, ROWS, BLK), F32),
-                pltpu.VMEM((4, ROWS, BLK), F32),
                 pltpu.VMEM((4, 8, 1, BLK), F32),
                 pltpu.VMEM((4, 4, 1, BLK), F32),
-                pltpu.VMEM((2, 8, 1, PLANE), F32),
-                pltpu.VMEM((2, 4, 1, PLANE), F32),
+                pltpu.VMEM((1, 8, 1, PLANE), F32),
+                pltpu.VMEM((1, 4, 1, PLANE), F32),
+                pltpu.VMEM((Q, 1, BLK), F32), pltpu.VMEM((32, 1, BLK), F32),
                 dma((Q,)), dma((Q, Q)), dma((2, Q)),
                 dma(()), dma((3,)), dma(()),
                 dma(()), dma((3,)), dma(()),
                 dma(()), dma((2, Q)), dma((Q,)),
                 dma((Q,)), dma((2, Q)), dma((Q,)),
-                dma((2, 6)), dma((6,)), dma((6,)),
+                dma((2, 5)), dma((5,)), dma((5,)),
                 dma(()), dma(()),
-                dma((Q + 1,)), dma((Q,)),
+                dma(()), dma(()), dma((Q + 1, Q)),
             ],
             compiler_params=pltpu.CompilerParams(
-                collective_id=0, has_side_effects=True, vmem_limit_bytes=67043328
+                collective_id=0, has_side_effects=True, vmem_limit_bytes=VMEM_BYTES
             ),
         )(init_blk, graph_blk)
-        return moved * scale
+        return result.reshape(init_blk.shape)
 
     return jax.shard_map(device_step, mesh=mesh, in_specs=(block_spec, block_spec), out_specs=block_spec, check_vma=False)

time: 191 us -> 187 us (0.979)
  other arithmetic: 3.16 us -> 0 us
  Pallas kernels: 188 us -> 186 us
    mul x1 -> x0, other arithmetic: 3.16 us -> none  [device_step(): return moved * scale]
where the time goes in v4:
time: 187 us
  Pallas kernels  186 us (99%)
    pallas_call x1, Pallas kernels, device_step(): pl.pallas_call(mcl_kernel, out_shape=pltpu.VMEM((Q, ROWS, BLK), F32), in_...  186 us

profile of v4, /device:TPU:1, one launch (start us, length us, event | category | flops | bytes accessed | tf_op | source)
XLA Modules:
  0.0 187.1 jit_solution(2258248598958140066)
XLA Ops:
  0.0 185.8 %shard_map.28 = f32[4,256,512]{2,1,0:T(8,128)S(1)} custom-call(f32[1024,512]{1,0:T(8,128)} %init_hbm.1, f32[1024,512]{1,0:T(8,128)} %graph_hbm.1), custom_call_target="tpu_custom_call" | custom-call | tf_op jit(solution)/shard_map/pallas_call | solution.py:513
  185.8 1.3 copy.4

commit v5 on v4

--- a/solution.py
+++ b/solution.py
@@ -17,7 +17,7 @@
 Q0, Q1, Q2, Q3 = range(Q)
 NEAR = (1, 3)
 XM, XP, YP = 224, 448, 736
-ROWS3 = ((0, 80), (80, 64), (144, 64), (208, 48))
+ROWS3 = ((0, 80), (80, 80), (160, 64), (224, 32))
 
 
 def mcl_kernel(
@@ -76,7 +76,7 @@
                     pltpu.make_async_copy(graph_hbm.at[rows, lanes], graph_ref.at[t, :, lanes], i_sem.at[q, t])
                 )
         copies.append(parts)
-    for q in (Q, Q0, Q1, Q2, Q3):
+    for q in (Q0, Q, Q1, Q2, Q3):
         for copy in copies[q]:
             copy.start()
 
@@ -90,14 +90,16 @@
                 block = graph_ref[yy * 2 + qr // 2, pl.ds(qr % 2 * LANE, LANE), lanes]
                 g[q, y, pl.ds(base + qr * ROWS + yy * LANE, LANE), :] = block.astype(BF)
 
+    def cast_init():
+        for copy in copies[Q]:
+            copy.wait()
+        for q in range(Q):
+            a[0, z, lax.div(y, 2), q, lax.rem(y, 2)] = init_ref[y, :, pl.ds(q * LANE, LANE)].astype(BF)
+        for t in range(Q):
+            for q in range(Q):
+                stage[t, q] = init_ref[t, :, pl.ds(q * LANE, LANE)].astype(BF)
+
     cast_graph(Q0)
-    for copy in copies[Q]:
-        copy.wait()
-    for q in range(Q):
-        a[0, z, lax.div(y, 2), q, lax.rem(y, 2)] = init_ref[y, :, pl.ds(q * LANE, LANE)].astype(BF)
-    for t in range(Q):
-        for q in range(Q):
-            stage[t, q] = init_ref[t, :, pl.ds(q * LANE, LANE)].astype(BF)
     pl.semaphore_wait(barrier, len(peers))
 
     def a0_block(dz, dy, lo=0, n=4):
@@ -319,12 +321,14 @@
         send(a2_rows(3, p, 0, 1), a2_rows(3, p, 0, 1), a2_send.at[p], a2_recv2.at[p], ZPOS)
         send(a2_rows(1, p, 1, 1), a2_rows(1, p, 1, 1), a2_send.at[p], a2_recv2.at[p], ZNEG)
 
-    def c3_part(zz, start, rows, nq):
+    def c3_part(zz, start, rows, nq, halves=(0, 1)):
         lhs = jnp.concatenate(
-            [a[2, zz, cc, qr, yy, pl.ds(start, rows), :] for cc in range(2) for qr in range(Q) for yy in range(2)],
+            [a[2, zz, cc, qr, yy, pl.ds(start, rows), :] for cc in halves for qr in range(Q) for yy in range(2)],
             axis=1,
         )
-        return jnp.dot(lhs, g_rows(nq, pl.multiple_of(zz * PLANE, PLANE), PLANE), preferred_element_type=F32)
+        depth = len(halves) * PIECE
+        base = pl.multiple_of(zz * PLANE + halves[0] * PIECE, PIECE)
+        return jnp.dot(lhs, g_rows(nq, base, depth), preferred_element_type=F32)
 
     def c3_own():
         def step(nq, carry):
@@ -333,16 +337,20 @@
 
         lax.fori_loop(0, 4, step, 0)
 
+    def c3_first(p, half=0):
+        start, rows = ROWS3[p]
+
+        def step(nq, carry):
+            part = c3_part(plus(z, 3), start, rows, nq, (half,))
+            acc1[nq, pl.ds(start, rows), :] += part + c3_part(plus(z, 1), start, rows, nq, (1 - half,))
+            return carry
+
+        lax.fori_loop(0, Q, step, 0)
+
     def c3_near(p):
         start, rows = ROWS3[p]
         await_recv(a.at[2, 0, :, :, :, pl.ds(start, rows), :], a2_recv.at[1, p])
-
-        def step(nq, carry):
-            acc1[nq, pl.ds(start, rows), :] += c3_part(plus(z, 1), start, rows, nq)
-            acc1[nq, pl.ds(start, rows), :] += c3_part(plus(z, 3), start, rows, nq)
-            return carry
-
-        lax.fori_loop(0, 4, step, 0)
+        c3_first(p, 1)
 
     def c3_far(p):
         start, rows = ROWS3[p]
@@ -387,82 +395,83 @@
             out_ref[t] = got[t] * scale
 
     g1(Q0)
-    a0_spread(0, (0,))
+    cast_init()
+    cast_graph(Q1)
+    g1(Q1)
     a0_exchange()
+    g2(Q0)
+    g2(Q1)
     cast_graph(Q2)
     g1(Q2)
-    g2(Q0)
+    a0_spread(0, (0,))
     a0_wait_near()
     a0_spread(1, NEAR)
-    cast_graph(Q1)
-    g1(Q1)
+    g3(Q0)
     a0_pass()
+    g3(Q1)
+    a0_relay(1, NEAR)
+    g4(Q0)
+    a0_relay(0, (0,))
     g2(Q2)
-    a0_relay(0, (0,))
-    g3(Q0)
-    g2(Q1)
     a0_wait_far()
     a0_spread(2, (2,))
-    a0_relay(1, NEAR)
+    g4(Q1)
     cast_graph(Q3)
     g1(Q3)
-    g4(Q0)
-    g3(Q1)
-    g3(Q2)
+    g_most(Q0)
     g5(Q0)
-    g_most(Q0)
     a0_relay(2, (2,))
     a0_done()
-    g4(Q1)
+    g_whole(Q0)
     c1_most(Q0)
-    g2(Q3)
-    g_whole(Q0)
     c1_rest(Q0)
     c1_sums(Q0)
-    g4(Q2)
+    g5(Q1)
     g_most(Q1)
+    g3(Q2)
+    g_whole(Q1)
     c1_most(Q1)
     c1_second(Q0)
-    g5(Q1)
-    g_whole(Q1)
     c1_rest(Q1)
     c1_sums(Q1)
-    g_most(Q2)
+    g2(Q3)
     a1_spread(Q0)
+    c1_second(Q1)
+    g4(Q2)
     g3(Q3)
     a1_relay(Q0)
-    c1_second(Q1)
     g5(Q2)
+    a1_spread(Q1)
+    g_whole(Q2)
+    g_most(Q2)
     c1_most(Q2)
-    g_whole(Q2)
     c1_rest(Q2)
     c1_sums(Q2)
-    a1_spread(Q1)
     g4(Q3)
     c1_second(Q2)
     a1_relay(Q1)
+    g_most(Q3)
+    c1_most(Q3)
+    g5(Q3)
     a1_spread(Q2)
-    g_most(Q3)
-    g5(Q3)
-    c1_most(Q3)
     g_whole(Q3)
     c1_rest(Q3)
     c1_sums(Q3)
-    c2(Q0, 0, True)
     c1_second(Q3)
     a1_relay(Q2)
-    c2_near(Q0)
+    c2(Q0, 0, True)
     a1_spread(Q3)
     c2(Q1, 0)
+    c2_near(Q0)
+    c2_far(Q0)
+    c2(Q2, 0)
+    c2_near(Q1)
+    a1_relay(Q3)
+    c2_far(Q1)
     c2_near(Q2)
-    c2_near(Q1)
-    c2_far(Q1)
-    a1_relay(Q3)
+    c2_near(Q3)
+    c2(Q3, 0)
     c2_far(Q2)
-    c2(Q3, 0)
-    c2_far(Q0)
-    c2_near(Q3)
-    c2(Q2, 0)
     c2_far(Q3)
     c2_sums()
     c2_second()
@@ -474,17 +483,21 @@
     c3_own()
     a2_relay(Q0)
     a2_spread(Q1)
+    c3_first(Q0)
     c3_near(Q0)
-    c3_far(Q0)
     a2_relay(Q1)
     a2_spread(Q2)
+    c3_far(Q0)
+    c3_first(Q1)
     c3_near(Q1)
-    c3_far(Q1)
     a2_relay(Q2)
     a2_spread(Q3)
+    c3_far(Q1)
+    c3_first(Q2)
+    a2_relay(Q3)
     c3_near(Q2)
     c3_far(Q2)
-    a2_relay(Q3)
+    c3_first(Q3)
     c3_near(Q3)
     c3_far(Q3)
     finish()

time: 187 us -> 182 us (0.973)
  Pallas kernels: 186 us -> 180 us
    pallas_call x1, Pallas kernels: 186 us -> 180 us  [device_step(): pl.pallas_call(mcl_kernel, out_shape=pltpu.VMEM((Q, ROWS, BLK), F32), in_...]
where the time goes in v5:
time: 182 us
  Pallas kernels  180 us (99%)
    pallas_call x1, Pallas kernels, device_step(): pl.pallas_call(mcl_kernel, out_shape=pltpu.VMEM((Q, ROWS, BLK), F32), in_...  180 us

profile of v5, /device:TPU:1, one launch (start us, length us, event | category | flops | bytes accessed | tf_op | source)
XLA Modules:
  0.0 181.5 jit_solution(14289344885123746873)
XLA Ops:
  0.0 180.2 %shard_map.28 = f32[4,256,512]{2,1,0:T(8,128)S(1)} custom-call(f32[1024,512]{1,0:T(8,128)} %init_hbm.1, f32[1024,512]{1,0:T(8,128)} %graph_hbm.1), custom_call_target="tpu_custom_call" | custom-call | tf_op jit(solution)/shard_map/pallas_call | solution.py:526
  180.2 1.3 copy.4

commit v6 on v5

--- a/solution.py
+++ b/solution.py
@@ -14,19 +14,20 @@
 N = 8192
 PLANE, PIECE, BLK, ROWS, LANE = 2048, 1024, 512, 256, 128
 Q = 4
-Q0, Q1, Q2, Q3 = range(Q)
+Q0, Q1, Q2, Q3, Q4 = range(Q + 1)
 NEAR = (1, 3)
 XM, XP, YP = 224, 448, 736
-ROWS3 = ((0, 80), (80, 80), (160, 64), (224, 32))
+EARLY = 32
+ROWS3 = ((0, EARLY), (32, 80), (112, 64), (176, 48), (224, 32))
 
 
 def mcl_kernel(
     init_hbm, graph_hbm, out_ref,
     moved, got,
-    g, a, stage, hold, acc1, acc2, s1a, s2a, s1b, s2b, s3, s4,
+    g, a, stage, hold, acc1, acc2, s1a, s2a, s1b, s2b, s3, s4, early, scales,
     g_send, g_recv, d_recv, t_send, t_recv, h_recv, az_send, az_recv, az2_recv,
     a1_send, a1_recv, a1_recv2, a2_send, a2_recv, a2_recv2,
-    r_send, r_recv1, r_recv2, o_send, o_recv, f_send, f_recv, i_sem,
+    r_send, r_recv1, r_recv2, e_send, e_recv, v_send, v_recv, o_send, o_recv, f_send, f_recv, i_sem,
 ):
     col, row = lax.axis_index("col"), lax.axis_index("row")
     z, y = lax.div(col, 4), lax.rem(col, 4)
@@ -297,18 +298,58 @@
     def c2_second():
         sum_second(s1b, s2b, 0, 4)
 
+    def early_part(dz, lo=0, n=2):
+        return early.at[plus(z, dz), pl.ds(lo, n)]
+
+    def early_spread():
+        for half in range(2):
+            for where, n in ((ZPOS, half), (ZNEG, 1 - half)):
+                src = acc2.at[pl.ds(2 * n, 2), pl.ds(0, EARLY), :]
+                send(src, early_part(0, 2 * n), e_send, e_recv.at[half], where)
+
+    def early_relay():
+        await_recv(early.at[0], e_recv.at[0])
+        send(early_part(3), early_part(3), e_send, e_recv.at[2], ZPOS)
+        send(early_part(1, 2), early_part(1, 2), e_send, e_recv.at[2], ZNEG)
+
+    def a2_scales():
+        sum_last(s2b, 0, Q)
+        scales[z] = N / jnp.sum(s2b[0], axis=0)
+        for dz in (2, 1, 3):
+            send(scales.at[z], scales.at[z], v_send, v_recv, dev(dz=dz))
+
+    def scaled(v, zz, q, t, rows):
+        lanes = pl.ds(q * BLK + t * LANE, LANE)
+        a[2, zz, t // 2, q, t % 2, rows, :] = (v * v * scales[zz, :, lanes]).astype(BF)
+
+    def early_scale(dz):
+        zz = plus(z, dz)
+        for q in range(Q):
+            for t in range(Q):
+                scaled(early[zz, q, :, pl.ds(t * LANE, LANE)], zz, q, t, pl.ds(0, EARLY))
+
+    def early_near():
+        await_recv(early.at[0], e_recv.at[1])
+        await_recv(scales.at[pl.ds(0, 3)], v_recv)
+        for dz in NEAR:
+            early_scale(dz)
+        for half in range(2):
+            c3_first(Q0, half)
+
+    def early_far():
+        await_recv(early.at[0], e_recv.at[2])
+        early_scale(2)
+        c3_far(Q0)
+
     def a2_rows(dz, p, lo=0, n=2):
         start, rows = ROWS3[p]
         return a.at[2, plus(z, dz), pl.ds(lo, n), :, :, pl.ds(start, rows), :]
 
     def a2_scale(p):
-        start, rows = ROWS3[p]
-        scale = N / jnp.sum(s2b[0], axis=0)
+        rows = pl.ds(*ROWS3[p])
         for q in range(Q):
             for t in range(Q):
-                v = acc2[q, pl.ds(start, rows), pl.ds(t * LANE, LANE)]
-                s = scale[:, q * BLK + t * LANE : q * BLK + t * LANE + LANE]
-                a[2, z, t // 2, q, t % 2, pl.ds(start, rows), :] = (v * v * s).astype(BF)
+                scaled(acc2[q, rows, pl.ds(t * LANE, LANE)], z, q, t, rows)
 
     def a2_spread(p):
         for half in range(2):
@@ -354,7 +395,8 @@
 
     def c3_far(p):
         start, rows = ROWS3[p]
-        await_recv(a.at[2, 0, :, :, :, pl.ds(start, rows), :], a2_recv2.at[p])
+        if p:
+            await_recv(a.at[2, 0, :, :, :, pl.ds(start, rows), :], a2_recv2.at[p])
         for nq in range(Q):
             v = acc1[nq, pl.ds(start, rows), :] + c3_part(plus(z, 2), start, rows, nq)
             v = v * v
@@ -367,7 +409,7 @@
                     s3[t, :, here] = part[:, cut]
                 else:
                     s3[t, :, here] += part[:, cut]
-        if p == Q3:
+        if p == Q4:
             c3_sums()
         for dy in (2, 1, 3):
             send(
@@ -473,33 +515,37 @@
     c2(Q3, 0)
     c2_far(Q2)
     c2_far(Q3)
+    early_spread()
     c2_sums()
     c2_second()
-    sum_last(s2b, 0, Q)
-    a2_scale(Q0)
-    a2_spread(Q0)
-    for p in (Q1, Q2, Q3):
+    early_relay()
+    a2_scales()
+    a2_scale(Q1)
+    a2_spread(Q1)
+    for p in (Q0, Q2, Q3, Q4):
         a2_scale(p)
     c3_own()
-    a2_relay(Q0)
-    a2_spread(Q1)
-    c3_first(Q0)
-    c3_near(Q0)
+    early_near()
     a2_relay(Q1)
     a2_spread(Q2)
-    c3_far(Q0)
+    early_far()
     c3_first(Q1)
     c3_near(Q1)
+    c3_far(Q1)
     a2_relay(Q2)
     a2_spread(Q3)
-    c3_far(Q1)
     c3_first(Q2)
-    a2_relay(Q3)
     c3_near(Q2)
     c3_far(Q2)
+    a2_relay(Q3)
+    a2_spread(Q4)
     c3_first(Q3)
     c3_near(Q3)
     c3_far(Q3)
+    a2_relay(Q4)
+    c3_first(Q4)
+    c3_near(Q4)
+    c3_far(Q4)
     finish()
 
     for q in range(Q):
@@ -507,7 +553,9 @@
     await_send(stage, t_send)
     await_send(a.at[0, pl.ds(0, 3)], az_send)
     await_send(a.at[1, pl.ds(0, 3)], a1_send)
-    for p, (start, rows) in enumerate(ROWS3):
+    await_send(early.at[pl.ds(0, 3)], e_send)
+    await_send(scales.at[pl.ds(0, 3)], v_send)
+    for p, (start, rows) in enumerate(ROWS3[1:], 1):
         await_send(a.at[2, pl.ds(0, 3), :, :, :, pl.ds(start, rows), :], a2_send.at[p])
     for s1, s2, base in ((s1a, s2a, 0), (s1b, s2b, 4)):
         for i in range(s1.shape[0]):
@@ -541,12 +589,14 @@
                 pltpu.VMEM((1, 8, 1, PLANE), F32),
                 pltpu.VMEM((1, 4, 1, PLANE), F32),
                 pltpu.VMEM((Q, 1, BLK), F32), pltpu.VMEM((32, 1, BLK), F32),
+                pltpu.VMEM((Q, Q, EARLY, BLK), F32), pltpu.VMEM((Q, 1, PLANE), F32),
                 dma((Q,)), dma((Q, Q)), dma((2, Q)),
                 dma(()), dma((3,)), dma(()),
                 dma(()), dma((3,)), dma(()),
                 dma(()), dma((2, Q)), dma((Q,)),
-                dma((Q,)), dma((2, Q)), dma((Q,)),
+                dma((Q + 1,)), dma((2, Q + 1)), dma((Q + 1,)),
                 dma((2, 5)), dma((5,)), dma((5,)),
+                dma(()), dma((3,)), dma(()), dma(()),
                 dma(()), dma(()),
                 dma(()), dma(()), dma((Q + 1, Q)),
             ],

time: 182 us -> 177 us (0.973)
  Pallas kernels: 180 us -> 175 us
    pallas_call x1, Pallas kernels: 180 us -> 175 us  [device_step(): pl.pallas_call(mcl_kernel, out_shape=pltpu.VMEM((Q, ROWS, BLK), F32), in_...]
where the time goes in v6:
time: 177 us; the launch traced here: 176 us
  Pallas kernels  175 us (99%)
    pallas_call x1, Pallas kernels, device_step(): pl.pallas_call(mcl_kernel, out_shape=pltpu.VMEM((Q, ROWS, BLK), F32), in_...  175 us

profile of v6, /device:TPU:1, one launch (start us, length us, event | category | flops | bytes accessed | tf_op | source)
XLA Modules:
  0.0 176.5 jit_solution(12165655732884269406)
XLA Ops:
  0.0 175.2 %shard_map.28 = f32[4,256,512]{2,1,0:T(8,128)S(1)} custom-call(f32[1024,512]{1,0:T(8,128)} %init_hbm.1, f32[1024,512]{1,0:T(8,128)} %graph_hbm.1), custom_call_target="tpu_custom_call" | custom-call | tf_op jit(solution)/shard_map/pallas_call | solution.py:574
  175.2 1.3 copy.4

commit v7 on v6

--- a/solution.py
+++ b/solution.py
@@ -14,11 +14,13 @@
 N = 8192
 PLANE, PIECE, BLK, ROWS, LANE = 2048, 1024, 512, 256, 128
 Q = 4
-Q0, Q1, Q2, Q3, Q4 = range(Q + 1)
+Q0, Q1, Q2, Q3 = range(Q)
 NEAR = (1, 3)
+FAR_FIRST = (2, 1, 3, 0)
+DIRECT = (Q2, Q3)
 XM, XP, YP = 224, 448, 736
 EARLY = 32
-ROWS3 = ((0, EARLY), (32, 80), (112, 64), (176, 48), (224, 32))
+ROWS3 = ((0, EARLY), (32, 80), (112, 96), (208, 48))
 
 
 def mcl_kernel(
@@ -27,7 +29,7 @@
     g, a, stage, hold, acc1, acc2, s1a, s2a, s1b, s2b, s3, s4, early, scales,
     g_send, g_recv, d_recv, t_send, t_recv, h_recv, az_send, az_recv, az2_recv,
     a1_send, a1_recv, a1_recv2, a2_send, a2_recv, a2_recv2,
-    r_send, r_recv1, r_recv2, e_send, e_recv, v_send, v_recv, o_send, o_recv, f_send, f_recv, i_sem,
+    r_send, r_recv1, r_recv2, e_send, e_recv, v_send, v_recv, o_send, o_recv, p_send, p_recv, i_sem,
 ):
     col, row = lax.axis_index("col"), lax.axis_index("row")
     z, y = lax.div(col, 4), lax.rem(col, 4)
@@ -233,33 +235,55 @@
 
     def sum_first(s1, i, k):
         me = x * 2 + c
-        for dx in range(Q):
+        for dx in FAR_FIRST:
             for dc in range(2):
-                if (dx, dc) != (0, 0):
+                if dx + dc:
                     send(s1.at[i, me], s1.at[i, me], r_send.at[0, k], r_recv1.at[k], dev(dx=dx, dc=dc))
 
     def sum_second(s1, s2, i, k):
         await_recv(s1.at[i, pl.ds(0, 7)], r_recv1.at[k])
         s2[i, y] = jnp.sum(s1[i], axis=0)
-        for dy in (1, 2, 3):
+        for dy in FAR_FIRST[:3]:
             send(s2.at[i, y], s2.at[i, y], r_send.at[1, k], r_recv2.at[k], dev(dy=dy))
 
     def sum_last(s2, i, k):
         await_recv(s2.at[i, pl.ds(0, 3)], r_recv2.at[k])
 
+    me_plane = y * 8 + x * 2 + c
+
+    def to_plane(source, dst, ssem, rsem):
+        for dy in FAR_FIRST:
+            for dx in FAR_FIRST:
+                for dc in range(2):
+                    if dx + dy + dc:
+                        send(source(dy), dst.at[me_plane], ssem, rsem, dev(dx=dx, dy=dy, dc=dc))
+
     def c1_sums(q):
-        s1a[q, x * 2 + c] = square_sum(acc1, q)
-        sum_first(s1a, q, q)
+        if q in DIRECT:
+            k = DIRECT.index(q)
+            s4[k, me_plane] = square_sum(acc1, q)
+            to_plane(lambda dy: s4.at[k, me_plane], s4.at[k], p_send.at[k], p_recv.at[k])
+        else:
+            s1a[q, x * 2 + c] = square_sum(acc1, q)
+            sum_first(s1a, q, q)
 
     def c1_second(q):
-        sum_second(s1a, s2a, q, q)
+        if q not in DIRECT:
+            sum_second(s1a, s2a, q, q)
+
+    def c1_scale(q):
+        if q in DIRECT:
+            k = DIRECT.index(q)
+            await_recv(s4.at[k, pl.ds(0, 31)], p_recv.at[k])
+            return N / jnp.sum(s4[k], axis=0)
+        sum_last(s2a, q, q)
+        return N / jnp.sum(s2a[q], axis=0)
 
     def a1_chunk(dz, q, lo=0, n=2):
         return a.at[1, plus(z, dz), pl.ds(lo, n), q]
 
     def a1_spread(q):
-        sum_last(s2a, q, q)
-        scale = N / jnp.sum(s2a[q], axis=0)
+        scale = c1_scale(q)
         for t in range(Q):
             v = acc1[q, :, pl.ds(t * LANE, LANE)]
             a[1, z, t // 2, q, t % 2] = (v * v * scale[:, t * LANE : t * LANE + LANE]).astype(BF)
@@ -409,7 +433,7 @@
                     s3[t, :, here] = part[:, cut]
                 else:
                     s3[t, :, here] += part[:, cut]
-        if p == Q4:
+        if p == Q3:
             c3_sums()
         for dy in (2, 1, 3):
             send(
@@ -419,17 +443,12 @@
             )
 
     def c3_sums():
-        me = y * 8 + x * 2 + c
-        s4[me] = s3[y]
-        for dy in (2, 1, 3, 0):
-            for dx in (2, 1, 3, 0):
-                for dc in range(2):
-                    if dx + dy + dc:
-                        send(s3.at[plus(y, dy)], s4.at[me], f_send, f_recv, dev(dx=dx, dy=dy, dc=dc))
+        to_plane(lambda dy: s3.at[plus(y, dy)], s4.at[2], p_send.at[2], p_recv.at[2])
+        s4[2, me_plane] = s3[y]
 
     def finish():
-        await_recv(s4.at[pl.ds(0, 31)], f_recv)
-        scale = N / jnp.sum(s4[...], axis=0)
+        await_recv(s4.at[2, pl.ds(0, 31)], p_recv.at[2])
+        scale = N / jnp.sum(s4[2], axis=0)
         out_ref[y] = moved[y] * scale
         await_recv(got.at[pl.ds(0, 3)], o_recv)
         for dy in (1, 2, 3):
@@ -522,7 +541,7 @@
     a2_scales()
     a2_scale(Q1)
     a2_spread(Q1)
-    for p in (Q0, Q2, Q3, Q4):
+    for p in (Q0, Q2, Q3):
         a2_scale(p)
     c3_own()
     early_near()
@@ -538,14 +557,9 @@
     c3_near(Q2)
     c3_far(Q2)
     a2_relay(Q3)
-    a2_spread(Q4)
     c3_first(Q3)
     c3_near(Q3)
     c3_far(Q3)
-    a2_relay(Q4)
-    c3_first(Q4)
-    c3_near(Q4)
-    c3_far(Q4)
     finish()
 
     for q in range(Q):
@@ -557,12 +571,13 @@
     await_send(scales.at[pl.ds(0, 3)], v_send)
     for p, (start, rows) in enumerate(ROWS3[1:], 1):
         await_send(a.at[2, pl.ds(0, 3), :, :, :, pl.ds(start, rows), :], a2_send.at[p])
-    for s1, s2, base in ((s1a, s2a, 0), (s1b, s2b, 4)):
-        for i in range(s1.shape[0]):
+    for s1, s2, base, n in ((s1a, s2a, 0, Q2), (s1b, s2b, Q, 1)):
+        for i in range(n):
             await_send(s1.at[i, pl.ds(0, 7)], r_send.at[0, base + i])
             await_send(s2.at[i, pl.ds(0, 3)], r_send.at[1, base + i])
     await_send(got.at[pl.ds(0, 3)], o_send)
-    await_send(s4.at[pl.ds(0, 31)], f_send)
+    for k in range(3):
+        await_send(s4.at[k, pl.ds(0, 31)], p_send.at[k])
 
 
 def solution(mesh):
@@ -588,17 +603,17 @@
                 pltpu.VMEM((4, 4, 1, BLK), F32),
                 pltpu.VMEM((1, 8, 1, PLANE), F32),
                 pltpu.VMEM((1, 4, 1, PLANE), F32),
-                pltpu.VMEM((Q, 1, BLK), F32), pltpu.VMEM((32, 1, BLK), F32),
+                pltpu.VMEM((Q, 1, BLK), F32), pltpu.VMEM((3, 32, 1, BLK), F32),
                 pltpu.VMEM((Q, Q, EARLY, BLK), F32), pltpu.VMEM((Q, 1, PLANE), F32),
                 dma((Q,)), dma((Q, Q)), dma((2, Q)),
                 dma(()), dma((3,)), dma(()),
                 dma(()), dma((3,)), dma(()),
                 dma(()), dma((2, Q)), dma((Q,)),
-                dma((Q + 1,)), dma((2, Q + 1)), dma((Q + 1,)),
+                dma((Q,)), dma((2, Q)), dma((Q,)),
                 dma((2, 5)), dma((5,)), dma((5,)),
                 dma(()), dma((3,)), dma(()), dma(()),
                 dma(()), dma(()),
-                dma(()), dma(()), dma((Q + 1, Q)),
+                dma((3,)), dma((3,)), dma((Q + 1, Q)),
             ],
             compiler_params=pltpu.CompilerParams(
                 collective_id=0, has_side_effects=True, vmem_limit_bytes=VMEM_BYTES

time: 177 us -> 176 us (level)
  no operation moved by 1% of the time
where the time goes in v7:
time: 176 us
  Pallas kernels  175 us (99%)
    pallas_call x1, Pallas kernels, device_step(): pl.pallas_call(mcl_kernel, out_shape=pltpu.VMEM((Q, ROWS, BLK), F32), in_...  175 us

profile of v7, /device:TPU:1, one launch (start us, length us, event | category | flops | bytes accessed | tf_op | source)
XLA Modules:
  0.0 176.2 jit_solution(10382367376580146525)
XLA Ops:
  0.0 174.9 %shard_map.28 = f32[4,256,512]{2,1,0:T(8,128)S(1)} custom-call(f32[1024,512]{1,0:T(8,128)} %init_hbm.1, f32[1024,512]{1,0:T(8,128)} %graph_hbm.1), custom_call_target="tpu_custom_call" | custom-call | tf_op jit(solution)/shard_map/pallas_call | solution.py:589
  174.9 1.3 copy.4

commit v8 on v7

--- a/solution.py
+++ b/solution.py
@@ -17,8 +17,8 @@
 Q0, Q1, Q2, Q3 = range(Q)
 NEAR = (1, 3)
 FAR_FIRST = (2, 1, 3, 0)
-DIRECT = (Q2, Q3)
-XM, XP, YP = 224, 448, 736
+XM, XP, YP, HALF = 112, 224, 368, 512
+LOW, HIGH = 0, 1
 EARLY = 32
 ROWS3 = ((0, EARLY), (32, 80), (112, 96), (208, 48))
 
@@ -26,10 +26,10 @@
 def mcl_kernel(
     init_hbm, graph_hbm, out_ref,
     moved, got,
-    g, a, stage, hold, acc1, acc2, s1a, s2a, s1b, s2b, s3, s4, early, scales,
+    g, a, stage, hold, acc1, acc2, s1b, s2b, s3, s4, early, scales,
     g_send, g_recv, d_recv, t_send, t_recv, h_recv, az_send, az_recv, az2_recv,
     a1_send, a1_recv, a1_recv2, a2_send, a2_recv, a2_recv2,
-    r_send, r_recv1, r_recv2, e_send, e_recv, v_send, v_recv, o_send, o_recv, p_send, p_recv, i_sem,
+    r_send, r_recv, e_send, e_recv, v_send, v_recv, o_send, o_recv, p_send, p_recv, i_sem,
 ):
     col, row = lax.axis_index("col"), lax.axis_index("row")
     z, y = lax.div(col, 4), lax.rem(col, 4)
@@ -60,8 +60,7 @@
         ).wait_send()
 
     barrier = pltpu.get_barrier_semaphore()
-    peers = [dev(dx=dx, dc=dc) for dx in range(Q) for dc in range(2) if (dx, dc) != (0, 0)]
-    peers += [dev(dy=dy) for dy in (1, 2, 3)] + [ZPOS, ZNEG]
+    peers = [XPOS, XNEG, YPOS, YNEG, ZPOS, ZNEG, MATE]
     for peer in peers:
         pl.semaphore_signal(barrier, inc=1, device_id=peer, device_id_type=MESH)
 
@@ -79,7 +78,7 @@
                     pltpu.make_async_copy(graph_hbm.at[rows, lanes], graph_ref.at[t, :, lanes], i_sem.at[q, t])
                 )
         copies.append(parts)
-    for q in (Q0, Q, Q1, Q2, Q3):
+    for q in (Q2, Q, Q0, Q1, Q3):
         for copy in copies[q]:
             copy.start()
 
@@ -102,7 +101,7 @@
             for q in range(Q):
                 stage[t, q] = init_ref[t, :, pl.ds(q * LANE, LANE)].astype(BF)
 
-    cast_graph(Q0)
+    cast_graph(Q2)
     pl.semaphore_wait(barrier, len(peers))
 
     def a0_block(dz, dy, lo=0, n=4):
@@ -142,66 +141,66 @@
             ref = a0_block(0, NEAR[1 - side], 2 * side, 2)
             send(hold.at[side], ref, t_send, t_recv.at[2], where)
 
-    def piece(q, dx, dy, lo=0, hi=PIECE):
-        base = (plus(x, dx) * 2 + c) * PIECE
+    def piece(q, h, dx, dy, lo=0, hi=HALF):
+        base = (plus(x, dx) * 2 + c) * PIECE + h * HALF
         return g.at[q, plus(y, dy), pl.ds(pl.multiple_of(base + lo, 16), hi - lo), :]
 
-    def hop(q, depth, where, dx, dy, lo=0, hi=PIECE):
-        ref = piece(q, dx, dy, lo, hi)
-        send(ref, ref, g_send.at[q], g_recv.at[q, depth], where)
-
-    def mate(q, *offsets, last=0):
+    def hop(q, h, depth, where, dx, dy, lo=0, hi=HALF):
+        ref = piece(q, h, dx, dy, lo, hi)
+        send(ref, ref, g_send.at[q], g_recv.at[q, h, depth], where)
+
+    def mate(q, h, offsets, last=0):
         for dx, dy in offsets:
-            ref = piece(q, dx, dy)
+            ref = piece(q, h, dx, dy)
             send(ref, ref, g_send.at[q], d_recv.at[last, q], MATE)
 
-    def arrived(q, depth):
-        rows = (4096, 2 * (BLK + 2 * (PIECE - XP)) + 2 * (BLK + 2 * XP), 4096, PIECE)[depth]
-        await_recv(g.at[q, 0, pl.ds(0, rows), :], g_recv.at[q, depth])
-
-    def g1(q):
+    def arrived(q, h, depth):
+        rows = (Q * HALF, 3 * PIECE, Q * HALF, HALF)[depth]
+        await_recv(g.at[q, 0, pl.ds(0, rows), :], g_recv.at[q, h, depth])
+
+    def g1(q, h):
         for where in (XPOS, XNEG, YPOS, YNEG):
-            hop(q, 0, where, 0, 0)
-        mate(q, (0, 0))
-
-    def g2(q):
-        arrived(q, 0)
-        hop(q, 1, XPOS, 3, 0, XM, YP)
-        hop(q, 1, YPOS, 0, 3, XM, YP)
-        for lo, hi in ((0, XM), (YP, PIECE)):
-            hop(q, 1, XNEG, 1, 0, lo, hi)
-            hop(q, 1, YNEG, 0, 1, lo, hi)
-        for d in (1, 3):
+            hop(q, h, 0, where, 0, 0)
+        mate(q, h, ((0, 0),))
+
+    def g2(q, h):
+        arrived(q, h, 0)
+        hop(q, h, 1, XPOS, 3, 0, XM, YP)
+        hop(q, h, 1, YPOS, 0, 3, XM, YP)
+        for lo, hi in ((0, XM), (YP, HALF)):
+            hop(q, h, 1, XNEG, 1, 0, lo, hi)
+            hop(q, h, 1, YNEG, 0, 1, lo, hi)
+        for d in NEAR:
             for where in (XPOS, XNEG):
-                hop(q, 1, where, 0, d, XP, PIECE)
+                hop(q, h, 1, where, 0, d, XP)
             for where in (YPOS, YNEG):
-                hop(q, 1, where, d, 0, 0, XP)
-        mate(q, (1, 0), (3, 0), (0, 1), (0, 3))
-
-    def g3(q):
-        arrived(q, 1)
+                hop(q, h, 1, where, d, 0, 0, XP)
+        mate(q, h, ((1, 0), (3, 0), (0, 1), (0, 3)))
+
+    def g3(q, h):
+        arrived(q, h, 1)
         for where in (XPOS, XNEG):
-            hop(q, 2, where, 0, 2, XP, PIECE)
+            hop(q, h, 2, where, 0, 2, XP)
         for where in (YPOS, YNEG):
-            hop(q, 2, where, 2, 0, 0, XP)
-        for d in (1, 3):
-            hop(q, 2, XPOS, 3, d, XP, YP)
-            hop(q, 2, XNEG, 1, d, YP, PIECE)
-            hop(q, 2, YPOS, d, 3, XM, XP)
-            hop(q, 2, YNEG, d, 1, 0, XM)
-        mate(q, (2, 0), (0, 2), (1, 1), (1, 3), (3, 1), (3, 3))
-
-    def g4(q):
-        arrived(q, 2)
-        hop(q, 3, XPOS, 3, 2, XP, YP)
-        hop(q, 3, XNEG, 1, 2, YP, PIECE)
-        hop(q, 3, YPOS, 2, 3, XM, XP)
-        hop(q, 3, YNEG, 2, 1, 0, XM)
-        mate(q, (1, 2), (3, 2), (2, 1), (2, 3))
-
-    def g5(q):
-        arrived(q, 3)
-        mate(q, (2, 2), last=1)
+            hop(q, h, 2, where, 2, 0, 0, XP)
+        for d in NEAR:
+            hop(q, h, 2, XPOS, 3, d, XP, YP)
+            hop(q, h, 2, XNEG, 1, d, YP)
+            hop(q, h, 2, YPOS, d, 3, XM, XP)
+            hop(q, h, 2, YNEG, d, 1, 0, XM)
+        mate(q, h, ((2, 0), (0, 2)) + tuple((i, j) for i in NEAR for j in NEAR))
+
+    def g4(q, h):
+        arrived(q, h, 2)
+        hop(q, h, 3, XPOS, 3, 2, XP, YP)
+        hop(q, h, 3, XNEG, 1, 2, YP)
+        hop(q, h, 3, YPOS, 2, 3, XM, XP)
+        hop(q, h, 3, YNEG, 2, 1, 0, XM)
+        mate(q, h, ((1, 2), (3, 2), (2, 1), (2, 3)))
+
+    def g5(q, h):
+        arrived(q, h, 3)
+        mate(q, h, ((2, 2),), last=1)
 
     def g_most(q):
         await_recv(g.at[q, pl.ds(0, 3), pl.ds(0, 5 * PIECE)], d_recv.at[0, q])
@@ -212,42 +211,49 @@
     def g_rows(nq, start, n):
         return jnp.concatenate([g[nq, t, pl.ds(start, n), :] for t in range(Q)], axis=1)
 
-    def c1_part(q, zz):
-        lhs = jnp.concatenate(
-            [a[0, zz, cc, qr, yy] for cc in range(2) for qr in range(Q) for yy in range(2)], axis=1
-        )
-        acc1[q] += jnp.dot(lhs, g_rows(q, pl.multiple_of(zz * PLANE, PLANE), PLANE), preferred_element_type=F32)
-
-    def c1_most(q):
+    def c1_part(q, zz, cc):
+        lhs = jnp.concatenate([a[0, zz, cc, qr, yy] for qr in range(Q) for yy in range(2)], axis=1)
+        base = pl.multiple_of(zz * PLANE + cc * PIECE, PIECE)
+        acc1[q] += jnp.dot(lhs, g_rows(q, base, PIECE), preferred_element_type=F32)
+
+    def c1_near(q, cc):
         def step(i, carry):
-            c1_part(q, plus(x, i + lax.div(i, 2)))
+            c1_part(q, plus(x, i + lax.div(i, 2)), cc)
             return carry
 
+        lax.fori_loop(0, 3, step, 0)
+
+    def c1_own(q):
         acc1[q] = jnp.zeros((ROWS, BLK), F32)
-        lax.fori_loop(0, 3, step, 0)
+        c1_near(q, c)
+
+    def c1_mate(q):
+        c1_near(q, 1 - c)
+
+    def c1_far(q):
+        c1_part(q, plus(x, 2), c)
 
     def c1_rest(q):
-        c1_part(q, plus(x, 2))
+        c1_part(q, plus(x, 2), 1 - c)
 
     def square_sum(ref, q):
         v = ref[q]
         return jnp.sum(v * v, axis=0, keepdims=True)
 
-    def sum_first(s1, i, k):
+    def c2_sums():
         me = x * 2 + c
+        for q in range(Q):
+            s1b[me, :, pl.ds(q * BLK, BLK)] = square_sum(acc2, q)
         for dx in FAR_FIRST:
             for dc in range(2):
                 if dx + dc:
-                    send(s1.at[i, me], s1.at[i, me], r_send.at[0, k], r_recv1.at[k], dev(dx=dx, dc=dc))
-
-    def sum_second(s1, s2, i, k):
-        await_recv(s1.at[i, pl.ds(0, 7)], r_recv1.at[k])
-        s2[i, y] = jnp.sum(s1[i], axis=0)
+                    send(s1b.at[me], s1b.at[me], r_send.at[0], r_recv.at[0], dev(dx=dx, dc=dc))
+
+    def c2_second():
+        await_recv(s1b.at[pl.ds(0, 7)], r_recv.at[0])
+        s2b[y] = jnp.sum(s1b[...], axis=0)
         for dy in FAR_FIRST[:3]:
-            send(s2.at[i, y], s2.at[i, y], r_send.at[1, k], r_recv2.at[k], dev(dy=dy))
-
-    def sum_last(s2, i, k):
-        await_recv(s2.at[i, pl.ds(0, 3)], r_recv2.at[k])
+            send(s2b.at[y], s2b.at[y], r_send.at[1], r_recv.at[1], dev(dy=dy))
 
     me_plane = y * 8 + x * 2 + c
 
@@ -259,25 +265,12 @@
                         send(source(dy), dst.at[me_plane], ssem, rsem, dev(dx=dx, dy=dy, dc=dc))
 
     def c1_sums(q):
-        if q in DIRECT:
-            k = DIRECT.index(q)
-            s4[k, me_plane] = square_sum(acc1, q)
-            to_plane(lambda dy: s4.at[k, me_plane], s4.at[k], p_send.at[k], p_recv.at[k])
-        else:
-            s1a[q, x * 2 + c] = square_sum(acc1, q)
-            sum_first(s1a, q, q)
-
-    def c1_second(q):
-        if q not in DIRECT:
-            sum_second(s1a, s2a, q, q)
+        s4[q, me_plane] = square_sum(acc1, q)
+        to_plane(lambda dy: s4.at[q, me_plane], s4.at[q], p_send.at[q], p_recv.at[q])
 
     def c1_scale(q):
-        if q in DIRECT:
-            k = DIRECT.index(q)
-            await_recv(s4.at[k, pl.ds(0, 31)], p_recv.at[k])
-            return N / jnp.sum(s4[k], axis=0)
-        sum_last(s2a, q, q)
-        return N / jnp.sum(s2a[q], axis=0)
+        await_recv(s4.at[q, pl.ds(0, 31)], p_recv.at[q])
+        return N / jnp.sum(s4[q], axis=0)
 
     def a1_chunk(dz, q, lo=0, n=2):
         return a.at[1, plus(z, dz), pl.ds(lo, n), q]
@@ -314,14 +307,6 @@
         await_recv(a.at[1, 0, :, 0], a1_recv2.at[q])
         c2(q, 2)
 
-    def c2_sums():
-        for q in range(Q):
-            s1b[0, x * 2 + c, :, pl.ds(q * BLK, BLK)] = square_sum(acc2, q)
-        sum_first(s1b, 0, 4)
-
-    def c2_second():
-        sum_second(s1b, s2b, 0, 4)
-
     def early_part(dz, lo=0, n=2):
         return early.at[plus(z, dz), pl.ds(lo, n)]
 
@@ -337,8 +322,8 @@
         send(early_part(1, 2), early_part(1, 2), e_send, e_recv.at[2], ZNEG)
 
     def a2_scales():
-        sum_last(s2b, 0, Q)
-        scales[z] = N / jnp.sum(s2b[0], axis=0)
+        await_recv(s2b.at[pl.ds(0, 3)], r_recv.at[1])
+        scales[z] = N / jnp.sum(s2b[...], axis=0)
         for dz in (2, 1, 3):
             send(scales.at[z], scales.at[z], v_send, v_recv, dev(dz=dz))
 
@@ -443,96 +428,120 @@
             )
 
     def c3_sums():
-        to_plane(lambda dy: s3.at[plus(y, dy)], s4.at[2], p_send.at[2], p_recv.at[2])
-        s4[2, me_plane] = s3[y]
+        to_plane(lambda dy: s3.at[plus(y, dy)], s4.at[Q], p_send.at[Q], p_recv.at[Q])
+        s4[Q, me_plane] = s3[y]
 
     def finish():
-        await_recv(s4.at[2, pl.ds(0, 31)], p_recv.at[2])
-        scale = N / jnp.sum(s4[2], axis=0)
+        await_recv(s4.at[Q, pl.ds(0, 31)], p_recv.at[Q])
+        scale = N / jnp.sum(s4[Q], axis=0)
         out_ref[y] = moved[y] * scale
         await_recv(got.at[pl.ds(0, 3)], o_recv)
         for dy in (1, 2, 3):
             t = plus(y, dy)
             out_ref[t] = got[t] * scale
 
-    g1(Q0)
+    g1(Q2, LOW)
+    cast_graph(Q1)
+    g1(Q1, HIGH)
+    cast_graph(Q0)
+    g1(Q0, HIGH)
     cast_init()
-    cast_graph(Q1)
-    g1(Q1)
     a0_exchange()
-    g2(Q0)
-    g2(Q1)
-    cast_graph(Q2)
-    g1(Q2)
+    g1(Q0, LOW)
+    g2(Q0, HIGH)
+    g1(Q1, LOW)
+    g2(Q1, HIGH)
     a0_spread(0, (0,))
+    g1(Q2, HIGH)
+    g2(Q0, LOW)
     a0_wait_near()
     a0_spread(1, NEAR)
-    g3(Q0)
+    g2(Q1, LOW)
+    a0_relay(0, (0,))
+    g3(Q1, HIGH)
     a0_pass()
-    g3(Q1)
+    g3(Q0, HIGH)
+    g3(Q0, LOW)
+    g3(Q1, LOW)
+    g2(Q2, HIGH)
     a0_relay(1, NEAR)
-    g4(Q0)
-    a0_relay(0, (0,))
-    g2(Q2)
     a0_wait_far()
     a0_spread(2, (2,))
-    g4(Q1)
+    g4(Q0, HIGH)
+    g4(Q1, HIGH)
+    g4(Q0, LOW)
+    g2(Q2, LOW)
+    g4(Q1, LOW)
+    g_most(Q1)
     cast_graph(Q3)
-    g1(Q3)
-    g_most(Q0)
-    g5(Q0)
+    g1(Q3, LOW)
     a0_relay(2, (2,))
     a0_done()
+    g3(Q2, HIGH)
+    c1_own(Q0)
+    g5(Q0, LOW)
+    g3(Q2, LOW)
+    g_most(Q0)
+    g5(Q1, LOW)
+    c1_mate(Q0)
+    g5(Q0, HIGH)
+    c1_far(Q0)
     g_whole(Q0)
-    c1_most(Q0)
     c1_rest(Q0)
     c1_sums(Q0)
-    g5(Q1)
-    g_most(Q1)
-    g3(Q2)
+    g1(Q3, HIGH)
+    g5(Q1, HIGH)
+    g4(Q2, HIGH)
+    g2(Q3, LOW)
+    c1_own(Q1)
+    c1_mate(Q1)
+    a1_spread(Q0)
     g_whole(Q1)
-    c1_most(Q1)
-    c1_second(Q0)
+    c1_far(Q1)
+    g5(Q2, HIGH)
     c1_rest(Q1)
     c1_sums(Q1)
-    g2(Q3)
-    a1_spread(Q0)
-    c1_second(Q1)
-    g4(Q2)
-    g3(Q3)
+    g4(Q2, LOW)
+    g2(Q3, HIGH)
+    c1_own(Q2)
+    g_most(Q2)
+    g5(Q2, LOW)
+    c1_mate(Q2)
+    c1_far(Q2)
     a1_relay(Q0)
-    g5(Q2)
-    a1_spread(Q1)
     g_whole(Q2)
-    g_most(Q2)
-    c1_most(Q2)
     c1_rest(Q2)
     c1_sums(Q2)
-    g4(Q3)
-    c1_second(Q2)
+    g3(Q3, LOW)
+    g3(Q3, HIGH)
+    a1_spread(Q1)
+    g4(Q3, LOW)
+    a1_spread(Q2)
     a1_relay(Q1)
+    g4(Q3, HIGH)
+    c1_own(Q3)
     g_most(Q3)
-    c1_most(Q3)
-    g5(Q3)
-    a1_spread(Q2)
+    g5(Q3, LOW)
+    g5(Q3, HIGH)
+    c1_far(Q3)
+    c1_mate(Q3)
     g_whole(Q3)
+    a1_relay(Q2)
     c1_rest(Q3)
     c1_sums(Q3)
-    c1_second(Q3)
-    a1_relay(Q2)
     c2(Q0, 0, True)
+    c2_near(Q1)
+    c2_near(Q0)
+    c2(Q2, 0)
     a1_spread(Q3)
+    a1_relay(Q3)
+    c2(Q3, 0)
+    c2_near(Q2)
     c2(Q1, 0)
-    c2_near(Q0)
+    c2_far(Q1)
+    c2_far(Q2)
     c2_far(Q0)
-    c2(Q2, 0)
-    c2_near(Q1)
-    a1_relay(Q3)
-    c2_far(Q1)
-    c2_near(Q2)
     c2_near(Q3)
-    c2(Q3, 0)
-    c2_far(Q2)
     c2_far(Q3)
     early_spread()
     c2_sums()
@@ -571,12 +580,10 @@
     await_send(scales.at[pl.ds(0, 3)], v_send)
     for p, (start, rows) in enumerate(ROWS3[1:], 1):
         await_send(a.at[2, pl.ds(0, 3), :, :, :, pl.ds(start, rows), :], a2_send.at[p])
-    for s1, s2, base, n in ((s1a, s2a, 0, Q2), (s1b, s2b, Q, 1)):
-        for i in range(n):
-            await_send(s1.at[i, pl.ds(0, 7)], r_send.at[0, base + i])
-            await_send(s2.at[i, pl.ds(0, 3)], r_send.at[1, base + i])
+    await_send(s1b.at[pl.ds(0, 7)], r_send.at[0])
+    await_send(s2b.at[pl.ds(0, 3)], r_send.at[1])
     await_send(got.at[pl.ds(0, 3)], o_send)
-    for k in range(3):
+    for k in range(Q + 1):
         await_send(s4.at[k, pl.ds(0, 31)], p_send.at[k])
 
 
@@ -599,21 +606,19 @@
                 pltpu.VMEM((2, 2, ROWS, LANE), BF),
                 pltpu.VMEM((4, ROWS, BLK), F32),
                 pltpu.VMEM((4, ROWS, BLK), F32),
-                pltpu.VMEM((4, 8, 1, BLK), F32),
-                pltpu.VMEM((4, 4, 1, BLK), F32),
-                pltpu.VMEM((1, 8, 1, PLANE), F32),
-                pltpu.VMEM((1, 4, 1, PLANE), F32),
-                pltpu.VMEM((Q, 1, BLK), F32), pltpu.VMEM((3, 32, 1, BLK), F32),
+                pltpu.VMEM((8, 1, PLANE), F32),
+                pltpu.VMEM((4, 1, PLANE), F32),
+                pltpu.VMEM((Q, 1, BLK), F32), pltpu.VMEM((Q + 1, 32, 1, BLK), F32),
                 pltpu.VMEM((Q, Q, EARLY, BLK), F32), pltpu.VMEM((Q, 1, PLANE), F32),
-                dma((Q,)), dma((Q, Q)), dma((2, Q)),
+                dma((Q,)), dma((Q, 2, Q)), dma((2, Q)),
                 dma(()), dma((3,)), dma(()),
                 dma(()), dma((3,)), dma(()),
                 dma(()), dma((2, Q)), dma((Q,)),
                 dma((Q,)), dma((2, Q)), dma((Q,)),
-                dma((2, 5)), dma((5,)), dma((5,)),
+                dma((2,)), dma((2,)),
                 dma(()), dma((3,)), dma(()), dma(()),
                 dma(()), dma(()),
-                dma((3,)), dma((3,)), dma((Q + 1, Q)),
+                dma((Q + 1,)), dma((Q + 1,)), dma((Q + 1, Q)),
             ],
             compiler_params=pltpu.CompilerParams(
                 collective_id=0, has_side_effects=True, vmem_limit_bytes=VMEM_BYTES

time: 176 us -> 176 us (level)
  no operation moved by 1% of the time
where the time goes in v8:
time: 176 us
  Pallas kernels  175 us (99%)
    pallas_call x1, Pallas kernels, device_step(): pl.pallas_call(mcl_kernel, out_shape=pltpu.VMEM((Q, ROWS, BLK), F32), in_...  175 us

profile of v8, /device:TPU:1, one launch (start us, length us, event | category | flops | bytes accessed | tf_op | source)
XLA Modules:
  0.0 176.2 jit_solution(10512480972675649923)
XLA Ops:
  0.0 174.8 %shard_map.28 = f32[4,256,512]{2,1,0:T(8,128)S(1)} custom-call(f32[1024,512]{1,0:T(8,128)} %init_hbm.1, f32[1024,512]{1,0:T(8,128)} %graph_hbm.1), custom_call_target="tpu_custom_call" | custom-call | tf_op jit(solution)/shard_map/pallas_call | solution.py:596
  174.9 1.3 copy.4

commit v9 on v7

--- a/solution.py
+++ b/solution.py
@@ -20,7 +20,7 @@
 DIRECT = (Q2, Q3)
 XM, XP, YP = 224, 448, 736
 EARLY = 32
-ROWS3 = ((0, EARLY), (32, 80), (112, 96), (208, 48))
+ROWS3 = ((0, EARLY), (32, 96), (128, 80), (208, 48))
 
 
 def mcl_kernel(
@@ -60,8 +60,7 @@
         ).wait_send()
 
     barrier = pltpu.get_barrier_semaphore()
-    peers = [dev(dx=dx, dc=dc) for dx in range(Q) for dc in range(2) if (dx, dc) != (0, 0)]
-    peers += [dev(dy=dy) for dy in (1, 2, 3)] + [ZPOS, ZNEG]
+    peers = [XPOS, XNEG, YPOS, YNEG, ZPOS, ZNEG, MATE]
     for peer in peers:
         pl.semaphore_signal(barrier, inc=1, device_id=peer, device_id_type=MESH)
 

time: 176 us -> 175 us (level)
  no operation moved by 1% of the time
where the time goes in v9:
time: 175 us
  Pallas kernels  174 us (99%)
    pallas_call x1, Pallas kernels, device_step(): pl.pallas_call(mcl_kernel, out_shape=pltpu.VMEM((Q, ROWS, BLK), F32), in_...  174 us

profile of v9, /device:TPU:1, one launch (start us, length us, event | category | flops | bytes accessed | tf_op | source)
XLA Modules:
  0.0 174.9 jit_solution(2890008674332977871)
XLA Ops:
  0.0 173.6 %shard_map.28 = f32[4,256,512]{2,1,0:T(8,128)S(1)} custom-call(f32[1024,512]{1,0:T(8,128)} %init_hbm.1, f32[1024,512]{1,0:T(8,128)} %graph_hbm.1), custom_call_target="tpu_custom_call" | custom-call | tf_op jit(solution)/shard_map/pallas_call | solution.py:588
  173.6 1.3 copy.4

commit v10 on v9

--- a/solution.py
+++ b/solution.py
@@ -20,7 +20,7 @@
 DIRECT = (Q2, Q3)
 XM, XP, YP = 224, 448, 736
 EARLY = 32
-ROWS3 = ((0, EARLY), (32, 96), (128, 80), (208, 48))
+ROWS3 = ((0, EARLY), (32, 112), (144, 64), (208, 48))
 
 
 def mcl_kernel(

time: 175 us -> 175 us (level)
  no operation moved by 1% of the time
where the time goes in v10:
time: 175 us
  Pallas kernels  173 us (99%)
    pallas_call x1, Pallas kernels, device_step(): pl.pallas_call(mcl_kernel, out_shape=pltpu.VMEM((Q, ROWS, BLK), F32), in_...  173 us

profile of v10, /device:TPU:1, one launch (start us, length us, event | category | flops | bytes accessed | tf_op | source)
XLA Modules:
  0.0 174.8 jit_solution(7912522563408215356)
XLA Ops:
  0.0 173.4 %shard_map.28 = f32[4,256,512]{2,1,0:T(8,128)S(1)} custom-call(f32[1024,512]{1,0:T(8,128)} %init_hbm.1, f32[1024,512]{1,0:T(8,128)} %graph_hbm.1), custom_call_target="tpu_custom_call" | custom-call | tf_op jit(solution)/shard_map/pallas_call | solution.py:588
  173.4 1.3 copy.4
